TPU v7x, 32 devices: a whole 2x2x4 slice. The times are simulated.
32 devices in a mesh: ty: 4 (over y, x), tx: 8 (over z, core).
Axes of the slice: x: 2, y: 2, z: 4, core: 2. Of those that a mesh axis runs over, the one named last changes fastest.
Arguments:
- sky: bfloat16 [2048, 4096], P('ty', 'tx'), may hold values from -6 to 6
- point_count: int32 [4, 8], P('ty', 'tx'), may hold values from 0 to 4, as said below
- point_offset: int32 [4, 8, 4, 2], P('ty', 'tx'), may hold values from 0 to 511
- beam_width: bfloat16 [4, 8, 4], P('ty', 'tx'), may hold values from 128 to 340
- uv_bins: int32 [4, 8, 4, 2, 2], P('ty', 'tx'), may hold values from 0 to 7
- uv_count: int32 [4, 8, 4], P('ty', 'tx'), may hold values from 1 to 2
- uv_weight: bfloat16 [4, 8, 4, 2, 128, 128], P('ty', 'tx'), may hold values from 1 to 8
Outputs:
- curvature: float32 [2048, 4096], P('ty', 'tx')
Inputs may be any that keep to these rules, and one draw needn't show every extreme that they name: `point_count`: each tile holds at most 4 pointings, and the tiles of columns 2i and 2i + 1 of one row hold at most 4 together; in every draw some such pair holds exactly 4, all on one of its tiles. `point_offset`: entries of slots at or beyond a tile's count are ignored. `uv_bins`: entries of uv slots at or beyond a pointing's uv_count are ignored.
All inputs are finite; a program needn't handle non-finite values.
Results may differ from a plain program's by a relative error of at most 0.0085.
Values may be sent and summed in bfloat16 or wider, within the bound.
A program may use at most 128 MiB of HBM per device.

v0:
```python
import math

import jax
import jax.numpy as jnp
from jax import lax
from jax.sharding import PartitionSpec as P


def padded(block, sides, width):
    for axis, dim in sides:
        count = lax.axis_size(axis)
        forward = [(i, i + 1) for i in range(count - 1)]
        backward = [(target, source) for source, target in forward]
        low = lax.ppermute(
            lax.slice_in_dim(block, block.shape[dim] - width, None, axis=dim), axis, forward
        )
        high = lax.ppermute(lax.slice_in_dim(block, 0, width, axis=dim), axis, backward)
        block = jnp.concatenate([low, block, high], axis=dim)
    return block


def swapped(x, axis, apart):
    return lax.ppermute(x, axis, [(i, i ^ 1 << apart) for i in range(lax.axis_size(axis))])


def shifted(value, axis, steps):
    count = lax.axis_size(axis)
    first, last = (max(0, -steps), min(count, count - steps))
    return lax.ppermute(value, axis, [(source, source + steps) for source in range(first, last)])


def for_sending(x):

    def short(part):
        return part.astype(jnp.bfloat16) if part.dtype == jnp.float32 else part

    return jax.tree.map(short, x)


def dft_tables(blocks, block_size, length):
    rows = blocks[:, None] * block_size + jnp.arange(block_size, dtype=jnp.int32)[None, :]
    pixels = jnp.arange(length, dtype=jnp.int32)
    phase = rows[:, :, None] * pixels[None, None, :] % length
    angle = phase.astype(jnp.float32) * (2.0 * math.pi / length)
    factor = 1.0 / math.sqrt(length)
    return (
        (jnp.cos(angle) * factor).astype(jnp.bfloat16),
        (jnp.sin(angle) * factor).astype(jnp.bfloat16),
    )


def beam_map(width, length):
    offset = jnp.arange(length, dtype=jnp.float32) - length // 2
    square = offset * offset
    radius = square[:, None] + square[None, :]
    spread = width.astype(jnp.float32)
    return jnp.exp(-radius / (2.0 * spread * spread))


def pointing_image(beamed, width, uv_pair, used, weight_tiles):
    slots_uv = weight_tiles.shape[0]
    block_size = weight_tiles.shape[1]
    length = beamed.shape[0]
    row_cos, row_sin = dft_tables(uv_pair[:, 0], block_size, length)
    col_cos, col_sin = dft_tables(uv_pair[:, 1], block_size, length)
    row_tables = jnp.stack([row_cos, row_sin], axis=1).reshape(slots_uv * 2 * block_size, length)
    col_tables = jnp.stack(
        [jnp.concatenate([col_cos, col_sin], axis=1), jnp.concatenate([-col_sin, col_cos], axis=1)],
        axis=1,
    )
    first = jnp.dot(row_tables, beamed, preferred_element_type=jnp.float32).astype(jnp.bfloat16)
    first = first.reshape(slots_uv, 2, block_size, length)
    visible = jnp.einsum("kcin,kcbn->kib", first, col_tables, preferred_element_type=jnp.float32)
    used_mask = (jnp.arange(slots_uv, dtype=jnp.int32) < used).astype(jnp.float32)
    weighted = weight_tiles.astype(jnp.float32) * used_mask[:, None, None]
    scaled = (visible * jnp.concatenate([weighted, weighted], axis=2)).astype(jnp.bfloat16)
    spread = jnp.einsum("kib,kcbn->kcin", scaled, col_tables, preferred_element_type=jnp.float32)
    spread = spread.astype(jnp.bfloat16).reshape(slots_uv * 2 * block_size, length)
    back = lax.dot_general(
        row_tables, spread, (((0,), (0,)), ((), ())), preferred_element_type=jnp.float32
    )
    return (beam_map(width, length) * back).astype(jnp.bfloat16)


def image_of(item):
    return pointing_image(item[0], item[1], item[2], item[3], item[4])


def add_patch(total, image, offset, live):
    patch_size = image.shape[0]
    current = lax.dynamic_slice(total, (offset[0], offset[1]), (patch_size, patch_size))
    update = jnp.where(live, image.astype(jnp.float32), jnp.zeros((), jnp.float32))
    return lax.dynamic_update_slice(total, current + update, (offset[0], offset[1]))


def shards(sky, point_count, point_offset, beam_width, uv_bins, uv_count, uv_weight):
    tile_size = sky.shape[0]
    patch_size = 2 * tile_size
    bordered = padded(sky, (("ty", 0), ("tx", 1)), tile_size)
    own_count = point_count[0, 0]
    offsets = point_offset[0, 0]
    widths = beam_width[0, 0]
    pair_bins = uv_bins[0, 0]
    used_counts = uv_count[0, 0]
    weight_tiles = uv_weight[0, 0]
    slots = offsets.shape[0]

    def beam_window(offset, width):
        window = lax.dynamic_slice(bordered, (offset[0], offset[1]), (patch_size, patch_size))
        return (beam_map(width, patch_size) * window.astype(jnp.float32)).astype(jnp.bfloat16)

    own_beamed = lax.map(lambda item: beam_window(item[0], item[1]), (offsets, widths))
    half_slots = slots // 2
    parity = lax.axis_index("tx") % 2
    first_slot = (1 - parity) * half_slots

    def pick(values):
        return lax.dynamic_slice_in_dim(values, first_slot, half_slots, 0)

    received = swapped(
        (
            pick(own_beamed),
            pick(widths),
            pick(pair_bins),
            pick(used_counts),
            pick(weight_tiles),
            point_count[0],
        ),
        "tx",
        0,
    )
    partner_count = received[5][0]
    first_count = jnp.where(parity == 0, own_count, partner_count)
    total_count = own_count + partner_count
    local_index = jnp.arange(half_slots, dtype=jnp.int32)
    combined = parity * half_slots + local_index
    even_side = combined < first_count
    pool_index = jnp.where(
        parity == 0,
        jnp.where(even_side, combined, slots + combined - first_count),
        jnp.where(even_side, slots + combined - half_slots, combined - first_count),
    )
    pool_index = jnp.clip(pool_index, 0, slots + half_slots - 1)

    def gather_pool(own_values, got_values):
        return jnp.take(jnp.concatenate([own_values, got_values], axis=0), pool_index, axis=0)

    items = (
        gather_pool(own_beamed, received[0]),
        gather_pool(widths, received[1]),
        gather_pool(pair_bins, received[2]),
        gather_pool(used_counts, received[3]),
        gather_pool(weight_tiles, received[4]),
    )
    images = lax.map(image_of, items)
    returned = swapped(images, "tx", 0)
    partner_combined = (1 - parity) * half_slots + local_index
    all_combined = jnp.concatenate([combined, partner_combined])
    all_images = jnp.concatenate([images, returned], axis=0)
    owner_odd = (all_combined >= first_count).astype(jnp.int32)
    slot_index = jnp.clip(all_combined - owner_odd * first_count, 0, slots - 1)
    live_flags = (owner_odd == parity) & (all_combined < total_count)
    placed = jnp.take(offsets, slot_index, axis=0)
    gathered = jnp.zeros((3 * tile_size, 3 * tile_size), jnp.float32)
    for position in range(all_images.shape[0]):
        gathered = add_patch(gathered, all_images[position], placed[position], live_flags[position])
    middle = gathered[:, tile_size : 2 * tile_size]
    middle = middle + shifted(gathered[:, :tile_size].astype(jnp.bfloat16), "tx", -1).astype(
        jnp.float32
    )
    middle = middle + shifted(gathered[:, 2 * tile_size :].astype(jnp.bfloat16), "tx", 1).astype(
        jnp.float32
    )
    result = middle[tile_size : 2 * tile_size, :]
    result = result + shifted(for_sending(middle[:tile_size, :]), "ty", -1)
    result = result + shifted(for_sending(middle[2 * tile_size :, :]), "ty", 1)
    return result


def solution(mesh):
    in_specs = (
        P("ty", "tx"),
        P("ty", "tx"),
        P("ty", "tx", None, None),
        P("ty", "tx", None),
        P("ty", "tx", None, None, None),
        P("ty", "tx", None),
        P("ty", "tx", None, None, None, None),
    )
    out_specs = P("ty", "tx")
    return jax.shard_map(shards, mesh=mesh, in_specs=in_specs, out_specs=out_specs, check_vma=False)
```

profile of v0, /device:TPU:21, one launch (start us, length us, event | category | flops | bytes accessed | tf_op | source)
XLA Modules:
  0.0 410.3 jit_solution(14474012761802401003)
XLA Ops:
  0.0 3.1 collective-permute-start.3
  3.1 3.1 collective-permute-start.4
  6.2 9.6 %collective-permute-done.3 = bf16[512,512]{1,0:T(8,128)(2,1)S(1)} collective-permute-done((bf16[512,512]{1,0:T(8,128)(2,1)}, bf16[512,512]{1,0:T(8,128)(2,1)S(1)}, u32[]{:S(2)}, u32[]{:S(2)}) %collective-permute-start.3) | collective-permute-done | bytes 524320 | tf_op jit(solution)/shard_map/ppermute | solution.py:14
  15.8 1.1 constant_dynamic-update-slice_fusion.1
  16.9 8.3 %collective-permute-done.4 = bf16[512,512]{1,0:T(8,128)(2,1)S(1)} collective-permute-done((bf16[512,512]{1,0:T(8,128)(2,1)}, bf16[512,512]{1,0:T(8,128)(2,1)S(1)}, u32[]{:S(2)}, u32[]{:S(2)}) %collective-permute-start.4) | collective-permute-done | bytes 524320 | tf_op jit(solution)/shard_map/ppermute | solution.py:17
  25.3 4.6 %collective-permute-start.5 = (bf16[1536,512]{1,0:T(8,128)(2,1)S(1)}, bf16[1536,512]{1,0:T(8,128)(2,1)S(1)}, u32[]{:S(2)}, u32[]{:S(2)}) collective-permute-start(bf16[1536,512]{1,0:T(8,128)(2,1)S(1)} %constant_dynamic-update-slice_fusion), channel_id=1, source_target_pairs={{0,1},{1,2},{2,3},{3,4},{4,5},{5,6},{6,7},{8,9},{9,10},{10,11},{11... | collective-permute-start | bytes 4718600 | tf_op jit(solution)/shard_map/ppermute | solution.py:14
  29.9 1.9 collective-permute-start.6
  31.9 15.3 %collective-permute-done.5 = bf16[1536,512]{1,0:T(8,128)(2,1)S(1)} collective-permute-done((bf16[1536,512]{1,0:T(8,128)(2,1)S(1)}, bf16[1536,512]{1,0:T(8,128)(2,1)S(1)}, u32[]{:S(2)}, u32[]{:S(2)}) %collective-permute-start.5) | collective-permute-done | bytes 1572896 | tf_op jit(solution)/shard_map/ppermute | solution.py:14
  47.3 4.5 %collective-permute-done.6 = bf16[1536,512]{1,0:T(8,128)(2,1)} collective-permute-done((bf16[1536,512]{1,0:T(8,128)(2,1)S(1)}, bf16[1536,512]{1,0:T(8,128)(2,1)}, u32[]{:S(2)}, u32[]{:S(2)}) %collective-permute-start.6) | collective-permute-done | bytes 1572896 | tf_op jit(solution)/shard_map/ppermute | solution.py:17
  51.8 3.4 pad_maximum_fusion.15
  55.2 45.2 %while.24 = (s32[]{:T(128)}, bf16[4,1024,1024]{2,1,0:T(8,128)(2,1)}, bf16[4]{0:T(256)(128)(2,1)S(1)}, s32[4,2]{0,1:T(2,128)S(1)}, bf16[1536,1536]{1,0:T(8,128)(2...) while((s32[]{:T(128)}, bf16[4,1024,1024]{2,1,0:T(8,128)(2,1)}, bf16[4]{0:T(256)(128)(2,1)S(1)}, ...), condition=%wide.region_1.2_spmd, body=%wide.region_0.1_spmd.sunk | while | flops 6293514 | bytes 4207341 | solution.py:112
  61.6 4.9 %fusion.67 = bf16[4,1024,1024]{2,1,0:T(8,128)(2,1)} fusion(bf16[4,1024,1024]{2,1,0:T(8,128)(2,1)} %get-tuple-element.338, s32[]{:T(128)} %get-tuple-element.337, bf16[1536,1536]{1,0:T(8,128)(2,1)} %get-tuple-element.350, s32[]{:T(128)S(6)} %select_n.387, s32[]{:T(128)S(6)} %select_n.388, f32[]{:T(128)S(6)} %mul.410, f32[1024]{0:T(1024)S(1)} %add_multiply_fusion.4), kind=kLoop, calls=%fused_computation.9.clone.1 | loop fusion | flops 6291456 | bytes 4203020 | tf_op jit(solution)/shard_map/while/body/jit(dynamic_update_index_in_dim)/dynamic_update_slice | solution.py:112
  72.9 4.9 %fusion.67 = bf16[4,1024,1024]{2,1,0:T(8,128)(2,1)} fusion(bf16[4,1024,1024]{2,1,0:T(8,128)(2,1)} %get-tuple-element.338, s32[]{:T(128)} %get-tuple-element.337, bf16[1536,1536]{1,0:T(8,128)(2,1)} %get-tuple-element.350, s32[]{:T(128)S(6)} %select_n.387, s32[]{:T(128)S(6)} %select_n.388, f32[]{:T(128)S(6)} %mul.410, f32[1024]{0:T(1024)S(1)} %add_multiply_fusion.4), kind=kLoop, calls=%fused_computation.9.clone.1 | loop fusion | flops 6291456 | bytes 4203020 | tf_op jit(solution)/shard_map/while/body/jit(dynamic_update_index_in_dim)/dynamic_update_slice | solution.py:112
  84.2 5.0 %fusion.67 = bf16[4,1024,1024]{2,1,0:T(8,128)(2,1)} fusion(bf16[4,1024,1024]{2,1,0:T(8,128)(2,1)} %get-tuple-element.338, s32[]{:T(128)} %get-tuple-element.337, bf16[1536,1536]{1,0:T(8,128)(2,1)} %get-tuple-element.350, s32[]{:T(128)S(6)} %select_n.387, s32[]{:T(128)S(6)} %select_n.388, f32[]{:T(128)S(6)} %mul.410, f32[1024]{0:T(1024)S(1)} %add_multiply_fusion.4), kind=kLoop, calls=%fused_computation.9.clone.1 | loop fusion | flops 6291456 | bytes 4203020 | tf_op jit(solution)/shard_map/while/body/jit(dynamic_update_index_in_dim)/dynamic_update_slice | solution.py:112
  95.5 4.9 %fusion.67 = bf16[4,1024,1024]{2,1,0:T(8,128)(2,1)} fusion(bf16[4,1024,1024]{2,1,0:T(8,128)(2,1)} %get-tuple-element.338, s32[]{:T(128)} %get-tuple-element.337, bf16[1536,1536]{1,0:T(8,128)(2,1)} %get-tuple-element.350, s32[]{:T(128)S(6)} %select_n.387, s32[]{:T(128)S(6)} %select_n.388, f32[]{:T(128)S(6)} %mul.410, f32[1024]{0:T(1024)S(1)} %add_multiply_fusion.4), kind=kLoop, calls=%fused_computation.9.clone.1 | loop fusion | flops 6291456 | bytes 4203020 | tf_op jit(solution)/shard_map/while/body/jit(dynamic_update_index_in_dim)/dynamic_update_slice | solution.py:112
  100.4 4.6 %constant_dynamic-slice_fusion.2 = bf16[2,1024,1024]{2,1,0:T(8,128)(2,1)} fusion(bf16[4,1024,1024]{2,1,0:T(8,128)(2,1)} %get-tuple-element.161, s32[]{:T(128)S(6)} %select_n.250), kind=kLoop, calls=%fused_computation.99 | loop fusion | bytes 8388612 | tf_op jit(solution)/shard_map/dynamic_slice | solution.py:118
  107.3 5.3 %collective-permute-done = s32[1]{0:T(128)} collective-permute-done((s32[1]{0:T(128)}, s32[1]{0:T(128)}, u32[]{:S(2)}, u32[]{:S(2)}) %collective-permute-start) | collective-permute-done | bytes 36 | tf_op jit(solution)/shard_map/ppermute | solution.py:23
  116.6 7.6 %constant_dynamic-update-slice_fusion.4 = bf16[6,1024,1024]{2,1,0:T(8,128)(2,1)} fusion(bf16[4,1024,1024]{2,1,0:T(8,128)(2,1)} %get-tuple-element.161), kind=kLoop, calls=%fused_computation.81 | loop fusion | bytes 16777216
  124.2 4.6 %constant_dynamic-update-slice_fusion.3 = bf16[6,1024,1024]{2,1,0:T(8,128)(2,1)} fusion(bf16[6,1024,1024]{2,1,0:T(8,128)(2,1)} %constant_dynamic-update-slice_fusion.4, bf16[2,1024,1024]{2,1,0:T(8,128)(2,1)} %collective-permute-done.7), kind=kLoop, calls=%fused_computation.80 | loop fusion | bytes 8388608 | tf_op jit(solution)/shard_map/concatenate | solution.py:146
  128.8 10.4 %fusion.49 = (bf16[6,512,1024]{2,1,0:T(8,128)(2,1)}, bf16[6,512,1024]{2,1,0:T(8,128)(2,1)}) fusion(bf16[6,1024,1024]{2,1,0:T(8,128)(2,1)} %constant_dynamic-update-slice_fusion.3), kind=kLoop, calls=%fused_computation.128 | loop fusion | bytes 25165824 | tf_op jit(solution)/shard_map/jit(_take)/gather | solution.py:146
  139.2 3.5 gather_fusion.5
  142.7 4.8 %gather_fusion.6 = bf16[2,512,1024]{2,1,0:T(8,128)(2,1)} fusion(bf16[6,512,1024]{2,1,0:T(8,128)(2,1)} %get-tuple-element.211, s32[1024]{0:T(1024)S(1)} %pad_clamp_fusion.1), kind=kCustom, calls=%fused_computation.6 | custom fusion | bytes 4194312 | tf_op jit(solution)/shard_map/jit(_take)/gather | solution.py:146
  147.5 4.0 maximum_select_fusion
  151.4 54.5 %while.25 = (s32[]{:T(128)}, bf16[2,1024,1024]{2,1,0:T(8,128)(2,1)}, bf16[2]{0:T(256)(128)(2,1)S(1)}, s32[2,2,2]{2,1,0:T(2,128)S(1)}, bf16[2,1024,1024]{2,1,0:T(...) while((s32[]{:T(128)}, bf16[2,1024,1024]{2,1,0:T(8,128)(2,1)}, ...), condition=%wide.region_3.4_spmd, body=%wide.region_2.3_spmd.sunk | while | flops 2712668672 | bytes 27871504 | solution.py:155
  151.7 4.9 %multiply_convert_fusion.8 = (bf16[2,128,1024]{2,1,0:T(8,128)(2,1)S(1)}, bf16[2,128,1024]{2,1,0:T(8,128)(2,1)S(1)}) fusion(s32[2,128]{1,0:T(2,128)S(1)} %get-tuple-element.323), kind=kLoop, calls=%fused_computation.42.clone.2 | loop fusion | flops 4718592 | bytes 1049600 | tf_op jit(solution)/shard_map/while/body/eval_jaxpr/convert_element_type | solution.py:48
  156.6 4.2 %fusion.73 = bf16[2,128,1024]{2,1,0:T(8,128)(2,1)S(1)} fusion(s32[2,128]{1,0:T(2,128)S(1)} %get-tuple-element.323), kind=kLoop, calls=%fused_computation.52.clone.1 | loop fusion | flops 4980736 | bytes 525312 | tf_op jit(solution)/shard_map/while/body/eval_jaxpr/neg | solution.py:68
  160.8 1.3 maximum_bitcast_fusion.3
  162.1 4.5 %multiply_convert_fusion.7 = (bf16[2,1,128,1024]{2,3,1,0:T(8,128)(2,1)S(1)}, bf16[2,1,128,1024]{2,3,1,0:T(8,128)(2,1)S(1)}) fusion(s32[2,128]{1,0:T(2,128)S(1)} %get-tuple-element.320), kind=kLoop, calls=%fused_computation.47.clone.1 | loop fusion | flops 4718592 | bytes 1049600 | tf_op jit(solution)/shard_map/while/body/eval_jaxpr/convert_element_type | solution.py:47
  166.7 1.3 copy.37
  168.0 3.2 fusion.72
  171.8 0.6 compare_convert_fusion.3
  172.6 0.8 fusion.74
  175.3 3.4 bitcast_dynamic-update-slice_fusion.2
  179.0 4.9 %multiply_convert_fusion.8 = (bf16[2,128,1024]{2,1,0:T(8,128)(2,1)S(1)}, bf16[2,128,1024]{2,1,0:T(8,128)(2,1)S(1)}) fusion(s32[2,128]{1,0:T(2,128)S(1)} %get-tuple-element.323), kind=kLoop, calls=%fused_computation.42.clone.2 | loop fusion | flops 4718592 | bytes 1049600 | tf_op jit(solution)/shard_map/while/body/eval_jaxpr/convert_element_type | solution.py:48
  183.9 4.2 %fusion.73 = bf16[2,128,1024]{2,1,0:T(8,128)(2,1)S(1)} fusion(s32[2,128]{1,0:T(2,128)S(1)} %get-tuple-element.323), kind=kLoop, calls=%fused_computation.52.clone.1 | loop fusion | flops 4980736 | bytes 525312 | tf_op jit(solution)/shard_map/while/body/eval_jaxpr/neg | solution.py:68
  188.1 1.3 maximum_bitcast_fusion.3
  189.4 4.5 %multiply_convert_fusion.7 = (bf16[2,1,128,1024]{2,3,1,0:T(8,128)(2,1)S(1)}, bf16[2,1,128,1024]{2,3,1,0:T(8,128)(2,1)S(1)}) fusion(s32[2,128]{1,0:T(2,128)S(1)} %get-tuple-element.320), kind=kLoop, calls=%fused_computation.47.clone.1 | loop fusion | flops 4718592 | bytes 1049600 | tf_op jit(solution)/shard_map/while/body/eval_jaxpr/convert_element_type | solution.py:47
  194.0 1.3 copy.37
  195.3 3.2 fusion.72
  199.1 0.6 compare_convert_fusion.3
  199.9 0.8 fusion.74
  202.6 3.4 bitcast_dynamic-update-slice_fusion.2
  207.7 0.7 fusion.52
  223.5 0.7 fusion.53
  224.2 4.8 %select_bitcast_fusion = f32[1024,1024]{1,0:T(8,128)} fusion(bf16[2,1024,1024]{2,1,0:T(8,128)(2,1)} %get-tuple-element.162, pred[]{:T(512)} %bitcast.25), kind=kLoop, calls=%fused_computation.69 | loop fusion | flops 2097152 | bytes 6291457 | tf_op jit(solution)/shard_map/jit(_where)/select_n | solution.py:92
  228.9 4.8 %broadcast_in_dim.77 = f32[1536,1536]{1,0:T(8,128)} broadcast(f32[]{:T(128)} %constant.209.clone.1), dimensions={} | broadcast | bytes 9437188 | tf_op jit(solution)/shard_map/broadcast_in_dim | solution.py:164
  233.8 24.4 %dynamic_update_slice.26 = f32[1536,1536]{1,0:T(8,128)} dynamic-update-slice(f32[1536,1536]{1,0:T(8,128)} %broadcast_in_dim.77, f32[1024,1024]{1,0:T(8,128)} %select_bitcast_fusion, s32[]{:T(128)S(6)} %select_n.266, s32[]{:T(128)S(6)} %select_n.267) | dynamic-update-slice | bytes 8388612 | tf_op jit(solution)/shard_map/dynamic_update_slice | solution.py:93
  258.2 6.8 %bitcast_add_fusion.2 = f32[1024,1024]{1,0:T(8,128)} fusion(f32[1536,1536]{1,0:T(8,128)} %dynamic_update_slice.26, s32[]{:T(128)S(6)} %select_n.268, s32[]{:T(128)S(6)} %select_n.269, bf16[2,1024,1024]{2,1,0:T(8,128)(2,1)} %get-tuple-element.162, pred[]{:T(512)} %bitcast.44), kind=kLoop, calls=%fused_computation.68 | loop fusion | flops 3145728 | bytes 10485769 | tf_op jit(solution)/shard_map/add | solution.py:93
  264.9 24.4 %dynamic_update_slice.27 = f32[1536,1536]{1,0:T(8,128)} dynamic-update-slice(f32[1536,1536]{1,0:T(8,128)} %dynamic_update_slice.26, f32[1024,1024]{1,0:T(8,128)} %bitcast_add_fusion.2, s32[]{:T(128)S(6)} %select_n.268, s32[]{:T(128)S(6)} %select_n.269) | dynamic-update-slice | bytes 8388612 | tf_op jit(solution)/shard_map/dynamic_update_slice | solution.py:93
  289.3 6.8 %bitcast_add_fusion.1 = f32[1024,1024]{1,0:T(8,128)} fusion(f32[1536,1536]{1,0:T(8,128)} %dynamic_update_slice.27, s32[]{:T(128)S(6)} %select_n.273, s32[]{:T(128)S(6)} %select_n.274, bf16[2,1024,1024]{2,1,0:T(8,128)(2,1)} %collective-permute-done.10, pred[]{:T(512)} %bitcast.48), kind=kLoop, calls=%fused_computation.67 | loop fusion | flops 3145728 | bytes 10485769 | tf_op jit(solution)/shard_map/add | solution.py:93
  296.1 24.4 %dynamic_update_slice.28 = f32[1536,1536]{1,0:T(8,128)} dynamic-update-slice(f32[1536,1536]{1,0:T(8,128)} %dynamic_update_slice.27, f32[1024,1024]{1,0:T(8,128)} %bitcast_add_fusion.1, s32[]{:T(128)S(6)} %select_n.273, s32[]{:T(128)S(6)} %select_n.274) | dynamic-update-slice | bytes 8388612 | tf_op jit(solution)/shard_map/dynamic_update_slice | solution.py:93
  320.5 6.8 %bitcast_add_fusion = f32[1024,1024]{1,0:T(8,128)} fusion(f32[1536,1536]{1,0:T(8,128)} %dynamic_update_slice.28, s32[]{:T(128)S(6)} %select_n.278, s32[]{:T(128)S(6)} %select_n.279, bf16[2,1024,1024]{2,1,0:T(8,128)(2,1)} %collective-permute-done.10, pred[]{:T(512)} %bitcast.52), kind=kLoop, calls=%fused_computation.66 | loop fusion | flops 3145728 | bytes 10485769 | tf_op jit(solution)/shard_map/add | solution.py:93
  327.3 24.4 %dynamic_update_slice.29 = f32[1536,1536]{1,0:T(8,128)} dynamic-update-slice(f32[1536,1536]{1,0:T(8,128)} %dynamic_update_slice.28, f32[1024,1024]{1,0:T(8,128)} %bitcast_add_fusion, s32[]{:T(128)S(6)} %select_n.278, s32[]{:T(128)S(6)} %select_n.279) | dynamic-update-slice | bytes 8388612 | tf_op jit(solution)/shard_map/dynamic_update_slice | solution.py:93
  351.7 4.3 %convert.11 = bf16[1536,1536]{1,0:T(8,128)(2,1)S(1)} convert(f32[1536,1536]{1,0:T(8,128)} %dynamic_update_slice.29) | non-fusion elementwise | flops 2359296 | bytes 14155776 | tf_op jit(solution)/shard_map/convert.6
  356.1 2.7 collective-permute-start.11
  358.8 2.9 collective-permute-start.12
  361.7 16.5 %collective-permute-done.11 = bf16[1536,512]{1,0:T(8,128)(2,1)S(1)} collective-permute-done((bf16[1536,512]{1,0:T(8,128)(2,1)S(1)}, bf16[1536,512]{1,0:T(8,128)(2,1)S(1)}, u32[]{:S(2)}, u32[]{:S(2)}) %collective-permute-start.11) | collective-permute-done | bytes 1572896 | tf_op jit(solution)/shard_map/ppermute | solution.py:29
  378.2 0.9 collective-permute-done.12
  379.1 2.7 fusion.46
  381.9 5.2 %collective-permute-start.13 = (bf16[512,512]{1,0:T(8,128)(2,1)S(1)}, bf16[512,512]{1,0:T(8,128)(2,1)S(1)}, u32[]{:S(2)}, u32[]{:S(2)}) collective-permute-start(bf16[512,512]{1,0:T(8,128)(2,1)S(1)} %get-tuple-element.214), channel_id=1, source_target_pairs={{8,0},{16,8},{24,16},{9,1},{17,9},{25,17},{10,2},{18,10},{26,18},{... | collective-permute-start | bytes 1572872 | tf_op jit(solution)/shard_map/ppermute | solution.py:29
  387.1 1.9 collective-permute-start.14
  389.0 8.2 %collective-permute-done.13 = bf16[512,512]{1,0:T(8,128)(2,1)S(1)} collective-permute-done((bf16[512,512]{1,0:T(8,128)(2,1)S(1)}, bf16[512,512]{1,0:T(8,128)(2,1)S(1)}, u32[]{:S(2)}, u32[]{:S(2)}) %collective-permute-start.13) | collective-permute-done | bytes 524320 | tf_op jit(solution)/shard_map/ppermute | solution.py:29
  397.2 11.9 %collective-permute-done.14 = bf16[512,512]{1,0:T(8,128)(2,1)S(1)} collective-permute-done((bf16[512,512]{1,0:T(8,128)(2,1)S(1)}, bf16[512,512]{1,0:T(8,128)(2,1)S(1)}, u32[]{:S(2)}, u32[]{:S(2)}) %collective-permute-start.14) | collective-permute-done | bytes 524320 | tf_op jit(solution)/shard_map/ppermute | solution.py:29
  409.1 1.2 fusion.33
  (95 shorter events, 14.7 us)
Async XLA Ops:
  0.0 15.8 %collective-permute-start.3 = (bf16[512,512]{1,0:T(8,128)(2,1)}, bf16[512,512]{1,0:T(8,128)(2,1)S(1)}, u32[]{:S(2)}, u32[]{:S(2)}) collective-permute-start(bf16[512,512]{1,0:T(8,128)(2,1)} %param.11), channel_id=1, source_target_pairs={{0,8},{8,16},{16,24},{1,9},{9,17},{17,25},{2,10},{10,18},{18,26},{... | collective-permute-start | bytes 1572872 | tf_op jit(solution)/shard_map/ppermute | solution.py:14
  3.1 22.1 %collective-permute-start.4 = (bf16[512,512]{1,0:T(8,128)(2,1)}, bf16[512,512]{1,0:T(8,128)(2,1)S(1)}, u32[]{:S(2)}, u32[]{:S(2)}) collective-permute-start(bf16[512,512]{1,0:T(8,128)(2,1)} %param.11), channel_id=1, source_target_pairs={{8,0},{16,8},{24,16},{9,1},{17,9},{25,17},{10,2},{18,10},{26,18},{... | collective-permute-start | bytes 1572872 | tf_op jit(solution)/shard_map/ppermute | solution.py:17
  25.3 22.0 %collective-permute-start.5 = (bf16[1536,512]{1,0:T(8,128)(2,1)S(1)}, bf16[1536,512]{1,0:T(8,128)(2,1)S(1)}, u32[]{:S(2)}, u32[]{:S(2)}) collective-permute-start(bf16[1536,512]{1,0:T(8,128)(2,1)S(1)} %constant_dynamic-update-slice_fusion), channel_id=1, source_target_pairs={{0,1},{1,2},{2,3},{3,4},{4,5},{5,6},{6,7},{8,9},{9,10},{10,11},{11... | collective-permute-start | bytes 4718600 | tf_op jit(solution)/shard_map/ppermute | solution.py:14
  29.9 21.8 %collective-permute-start.6 = (bf16[1536,512]{1,0:T(8,128)(2,1)S(1)}, bf16[1536,512]{1,0:T(8,128)(2,1)}, u32[]{:S(2)}, u32[]{:S(2)}) collective-permute-start(bf16[1536,512]{1,0:T(8,128)(2,1)S(1)} %constant_dynamic-update-slice_fusion), channel_id=1, source_target_pairs={{1,0},{2,1},{3,2},{4,3},{5,4},{6,5},{7,6},{9,8},{10,9},{11,10},{12... | collective-permute-start | bytes 4718600 | tf_op jit(solution)/shard_map/ppermute | solution.py:17
  31.9 23.3 %copy-start.2 = (s32[1,1,4,2]{2,3,1,0:T(2,128)S(1)}, s32[1,1,4,2]{2,3,1,0:T(2,128)}, u32[]{:S(2)}) copy-start(s32[1,1,4,2]{2,3,1,0:T(2,128)} %param.13) | copy-start | bytes 100
  31.9 23.3 %copy-start.4 = (bf16[1,1,4]{2,1,0:T(2,128)(2,1)S(1)}, bf16[1,1,4]{2,1,0:T(2,128)(2,1)}, u32[]{:S(2)}) copy-start(bf16[1,1,4]{2,1,0:T(2,128)(2,1)} %param.14) | copy-start | bytes 28
  100.4 5.2 %copy-start.5 = (s32[1,1,4]{2,1,0:T(1,128)S(1)}, s32[1,1,4]{2,1,0:T(1,128)}, u32[]{:S(2)}) copy-start(s32[1,1,4]{2,1,0:T(1,128)} %param.16) | copy-start | bytes 52
  100.4 5.2 %copy-start.1 = (bf16[1,1,4,2,128,128]{5,4,3,2,1,0:T(8,128)(2,1)S(1)}, bf16[1,1,4,2,128,128]{5,4,3,2,1,0:T(8,128)(2,1)}, u32[]{:S(2)}) copy-start(bf16[1,1,4,2,128,128]{5,4,3,2,1,0:T(8,128)(2,1)} %param.17) | copy-start | bytes 786436
  100.4 5.8 %copy-start.3 = (s32[1,1,4,2,2]{2,4,3,1,0:T(2,128)S(1)}, s32[1,1,4,2,2]{2,4,3,1,0:T(2,128)}, u32[]{:S(2)}) copy-start(s32[1,1,4,2,2]{2,4,3,1,0:T(2,128)} %param.15) | copy-start | bytes 196
  105.0 19.2 %collective-permute-start.7 = (bf16[2,1024,1024]{2,1,0:T(8,128)(2,1)}, bf16[2,1024,1024]{2,1,0:T(8,128)(2,1)}, u32[]{:S(2)}, u32[]{:S(2)}) collective-permute-start(bf16[2,1024,1024]{2,1,0:T(8,128)(2,1)} %constant_dynamic-slice_fusion.2), channel_id=1, source_target_pairs={{0,1},{1,0},{2,3},{3,2},{4,5},{5,4},{6,7},{7,6},{8,9},{9,8},{10,11... | collective-permute-start | bytes 12582920 | tf_op jit(solution)/shard_map/ppermute | solution.py:23
  105.0 7.5 %collective-permute-start = (s32[1]{0:T(128)}, s32[1]{0:T(128)}, u32[]{:S(2)}, u32[]{:S(2)}) collective-permute-start(s32[1]{0:T(128)} %bitcast.23), channel_id=1, source_target_pairs={{0,1},{1,0},{2,3},{3,2},{4,5},{5,4},{6,7},{7,6},{8,9},{9,8},{10,11... | collective-permute-start | bytes 20 | tf_op jit(solution)/shard_map/ppermute | solution.py:23
  105.6 8.8 %collective-permute-start.9 = (s32[2]{0:T(128)S(1)}, s32[2]{0:T(128)S(1)}, u32[]{:S(2)}, u32[]{:S(2)}) collective-permute-start(s32[2]{0:T(128)S(1)} %fusion.41), channel_id=1, source_target_pairs={{0,1},{1,0},{2,3},{3,2},{4,5},{5,4},{6,7},{7,6},{8,9},{9,8},{10,11... | collective-permute-start | bytes 32 | tf_op jit(solution)/shard_map/ppermute | solution.py:23
  105.7 10.2 %collective-permute-start.8 = (bf16[2,2,128,128]{3,2,1,0:T(8,128)(2,1)S(1)}, bf16[2,2,128,128]{3,2,1,0:T(8,128)(2,1)S(1)}, u32[]{:S(2)}, u32[]{:S(2)}) collective-permute-start(bf16[2,2,128,128]{3,2,1,0:T(8,128)(2,1)S(1)} %dynamic-slice_bitcast_fusion.1), channel_id=1, source_target_pairs={{0,1},{1,0},{2,3},{3,2},{4,5},{5,4},{6,7},{7,6},{8,9},{9,8},{10,11... | collective-permute-start | bytes 393224 | tf_op jit(solution)/shard_map/ppermute | solution.py:23
  106.4 8.8 %collective-permute-start.2 = (s32[2,2,2]{2,1,0:T(2,128)S(1)}, s32[2,2,2]{2,1,0:T(2,128)S(1)}, u32[]{:S(2)}, u32[]{:S(2)}) collective-permute-start(s32[2,2,2]{2,1,0:T(2,128)S(1)} %bitcast.148), channel_id=1, source_target_pairs={{0,1},{1,0},{2,3},{3,2},{4,5},{5,4},{6,7},{7,6},{8,9},{9,8},{10,11... | collective-permute-start | bytes 104 | tf_op jit(solution)/shard_map/ppermute | solution.py:23
  112.5 1.2 collective-permute-start.1
  168.0 4.6 %copy-start = (bf16[2,1,256,1024]{3,2,1,0:T(8,128)(2,1)S(1)}, bf16[2,1,256,1024]{3,2,1,0:T(8,128)(2,1)}, u32[]{:S(2)}) copy-start(bf16[2,1,256,1024]{3,2,1,0:T(8,128)(2,1)} %get-tuple-element.326) | copy-start | bytes 3145732 | tf_op jit(solution)/shard_map/while
  195.3 4.6 %copy-start = (bf16[2,1,256,1024]{3,2,1,0:T(8,128)(2,1)S(1)}, bf16[2,1,256,1024]{3,2,1,0:T(8,128)(2,1)}, u32[]{:S(2)}) copy-start(bf16[2,1,256,1024]{3,2,1,0:T(8,128)(2,1)} %get-tuple-element.326) | copy-start | bytes 3145732 | tf_op jit(solution)/shard_map/while
  206.0 83.3 %collective-permute-start.10 = (bf16[2,1024,1024]{2,1,0:T(8,128)(2,1)}, bf16[2,1024,1024]{2,1,0:T(8,128)(2,1)}, u32[]{:S(2)}, u32[]{:S(2)}) collective-permute-start(bf16[2,1024,1024]{2,1,0:T(8,128)(2,1)} %get-tuple-element.162), channel_id=1, source_target_pairs={{0,1},{1,0},{2,3},{3,2},{4,5},{5,4},{6,7},{7,6},{8,9},{9,8},{10,11... | collective-permute-start | bytes 12582920 | tf_op jit(solution)/shard_map/ppermute | solution.py:23
  356.1 22.0 %collective-permute-start.11 = (bf16[1536,512]{1,0:T(8,128)(2,1)S(1)}, bf16[1536,512]{1,0:T(8,128)(2,1)S(1)}, u32[]{:S(2)}, u32[]{:S(2)}) collective-permute-start(bf16[1536,512]{1,0:T(8,128)(2,1)S(1)} %get-tuple-element.212), channel_id=1, source_target_pairs={{1,0},{2,1},{3,2},{4,3},{5,4},{6,5},{7,6},{9,8},{10,9},{11,10},{12... | collective-permute-start | bytes 4718600 | tf_op jit(solution)/shard_map/ppermute | solution.py:29
  358.8 20.2 %collective-permute-start.12 = (bf16[1536,512]{1,0:T(8,128)(2,1)S(1)}, bf16[1536,512]{1,0:T(8,128)(2,1)S(1)}, u32[]{:S(2)}, u32[]{:S(2)}) collective-permute-start(bf16[1536,512]{1,0:T(8,128)(2,1)S(1)} %get-tuple-element.213), channel_id=1, source_target_pairs={{0,1},{1,2},{2,3},{3,4},{4,5},{5,6},{6,7},{8,9},{9,10},{10,11},{11... | collective-permute-start | bytes 4718600 | tf_op jit(solution)/shard_map/ppermute | solution.py:29
  381.9 15.3 %collective-permute-start.13 = (bf16[512,512]{1,0:T(8,128)(2,1)S(1)}, bf16[512,512]{1,0:T(8,128)(2,1)S(1)}, u32[]{:S(2)}, u32[]{:S(2)}) collective-permute-start(bf16[512,512]{1,0:T(8,128)(2,1)S(1)} %get-tuple-element.214), channel_id=1, source_target_pairs={{8,0},{16,8},{24,16},{9,1},{17,9},{25,17},{10,2},{18,10},{26,18},{... | collective-permute-start | bytes 1572872 | tf_op jit(solution)/shard_map/ppermute | solution.py:29
  387.1 22.0 %collective-permute-start.14 = (bf16[512,512]{1,0:T(8,128)(2,1)S(1)}, bf16[512,512]{1,0:T(8,128)(2,1)S(1)}, u32[]{:S(2)}, u32[]{:S(2)}) collective-permute-start(bf16[512,512]{1,0:T(8,128)(2,1)S(1)} %get-tuple-element.215), channel_id=1, source_target_pairs={{0,8},{8,16},{16,24},{1,9},{9,17},{17,25},{2,10},{10,18},{18,26},{... | collective-permute-start | bytes 1572872 | tf_op jit(solution)/shard_map/ppermute | solution.py:29
where the time goes:
time: 417 us; the launch traced here: 410 us
  local copies, waits for them, and re-layouts  154 us (37%)
  other arithmetic  93 us (22%)
  waiting for transfers between devices  80.9 us (19%)
  starting transfers between devices  26.8 us (6%)
  loops' own time  23.1 us (6%)
  between operations  17.3 us (4%)
  matrix products  14.9 us (4%)
    dynamic_update_slice x4, local copies, waits for them, and re-layouts, add_patch(): lax.dynamic_update_slice(total, current + update, (offset[0], offset[1]))  97.6 us
    ppermute x4, waiting for transfers between devices, shifted(): lax.ppermute(value, axis, [(source, source + steps) for source in range(f...  37.4 us
    ppermute x2, waiting for transfers between devices, padded(): lax.ppermute(lax.slice_in_dim(block, block.shape[dim] - width, None, axis...  25 us
    gather x7, local copies, waits for them, and re-layouts, gather_pool(): jnp.take(jnp.concatenate([own_values, got_values], axis=0), pool_index, a...  21.1 us
    another operation x1, loops' own time, shards(): lax.map(lambda item: beam_window(item[0], item[1]), (offsets, widths))  20.4 us
    add x3, other arithmetic, add_patch(): current + update  20.3 us
    dynamic_update_slice x4, other arithmetic, shards(): lax.map(lambda item: beam_window(item[0], item[1]), (offsets, widths))  19.7 us
    ppermute x2, waiting for transfers between devices, padded(): lax.ppermute(lax.slice_in_dim(block, 0, width, axis=dim), axis, backward)  12.8 us
  transfers between devices with their start and end apart: 15, of which 10 were waited for; matrix products, arithmetic and copies ran while one was open for 19% of the time, Pallas kernels for 0%

commit v1 on v0

v1 whole, which is shorter than its diff:
```python
import functools
import math

import jax
import jax.numpy as jnp
from jax import lax
from jax.experimental import pallas as pl
from jax.experimental.pallas import tpu as pltpu
from jax.sharding import PartitionSpec as P

F32 = jnp.float32
BF16 = jnp.bfloat16
CHUNK = 256


def shifted(value, axis, steps):
    count = lax.axis_size(axis)
    first, last = (max(0, -steps), min(count, count - steps))
    return lax.ppermute(value, axis, [(source, source + steps) for source in range(first, last)])


def full_tables(length):
    index = jnp.arange(length, dtype=jnp.int32)
    phase = index[:, None] * index[None, :] % length
    angle = phase.astype(F32) * (2.0 * math.pi / length)
    factor = 1.0 / math.sqrt(length)
    return (jnp.cos(angle) * factor).astype(BF16), (jnp.sin(angle) * factor).astype(BF16)


def gaussians(start, decay, size, axis):
    shape = (size, 128) if axis == 0 else (8, size)
    index = lax.broadcasted_iota(jnp.int32, shape, axis)

    def value(pixel):
        away = (pixel - start - size).astype(F32)
        return jnp.exp(-(away * away) * decay)

    zero = jnp.zeros(shape, F32)
    low = jnp.where(index >= start, value(index), zero)
    high = jnp.where(index < start, value(index + 2 * size), zero)
    return low, value(index + size), high


def wide(column, width):
    return jnp.concatenate([column] * (width // 128), axis=1)


def beams(p, off_ref, decay_ref, gy_ref, gx_ref, size):
    decay = decay_ref[p]
    for part, values in enumerate(gaussians(off_ref[p, 0], decay, size, 0)):
        gy_ref[part] = values
    for part, values in enumerate(gaussians(off_ref[p, 1], decay, size, 1)):
        gx_ref[part] = values


def row_tables(p, bins_ref, which, cos_ref, sin_ref, rows_ref, block, slots_uv):
    for k in range(slots_uv):
        at = pl.ds(pl.multiple_of(bins_ref[p, 2 * k + which] * block, block), block)
        rows_ref[(2 * k) * block : (2 * k + 1) * block, :] = cos_ref[at, :]
        rows_ref[(2 * k + 1) * block : (2 * k + 2) * block, :] = sin_ref[at, :]


def flipped_tables(p, bins_ref, cos_ref, sin_ref, flip_ref, block, slots_uv):
    for k in range(slots_uv):
        at = pl.ds(pl.multiple_of(bins_ref[p, 2 * k] * block, block), block)
        flip_ref[:, (2 * k) * block : (2 * k + 1) * block] = cos_ref[:, at]
        flip_ref[:, (2 * k + 1) * block : (2 * k + 2) * block] = sin_ref[:, at]


def early_kernel(
    count_ref, off_ref, bins_ref, decay_ref, cos_ref, sin_ref, up_ref, own_ref, down_ref,
    first_ref, gy_ref, gx_ref, rows_ref, beamed_ref,
):
    size = own_ref.shape[0]
    block = rows_ref.shape[0] // bins_ref.shape[1]
    slots_uv = bins_ref.shape[1] // 2

    def step(p, carry):
        beams(p, off_ref, decay_ref, gy_ref, gx_ref, size)
        row_tables(p, bins_ref, 0, cos_ref, sin_ref, rows_ref, block, slots_uv)
        for at in range(0, size, CHUNK):
            cols = slice(at, at + CHUNK)
            gx = gx_ref[1, 0:1, cols]
            top = wide(gy_ref[0], CHUNK) * up_ref[:, cols].astype(F32)
            top = top + wide(gy_ref[2], CHUNK) * down_ref[:, cols].astype(F32)
            beamed_ref[:size, cols] = (gx * top).astype(BF16)
            low = wide(gy_ref[1], CHUNK) * own_ref[:, cols].astype(F32)
            beamed_ref[size:, cols] = (gx * low).astype(BF16)
        for at in range(0, size, CHUNK):
            cols = slice(at, at + CHUNK)
            first_ref[p, :, cols] = jnp.dot(
                rows_ref[...], beamed_ref[:, cols], preferred_element_type=F32
            ).astype(BF16)
        return carry

    lax.fori_loop(0, count_ref[0], step, 0)


def middle_kernel(
    count_ref, off_ref, bins_ref, used_ref, decay_ref, cos_ref, sin_ref, weight_ref, early_ref,
    ul_ref, l_ref, dl_ref, ur_ref, r_ref, dr_ref,
    oul_ref, ol_ref, odl_ref, our_ref, or_ref, odr_ref, late_ref,
    gy_ref, gx_ref, rows_ref, cols_ref, flip_ref, beamed_ref, first_ref, spread_ref, acc_ref,
):
    size = l_ref.shape[0]
    block = rows_ref.shape[0] // bins_ref.shape[1]
    slots_uv = bins_ref.shape[1] // 2
    pair = 2 * block
    acc_ref[...] = jnp.zeros_like(acc_ref)

    def step(p, carry):
        beams(p, off_ref, decay_ref, gy_ref, gx_ref, size)
        row_tables(p, bins_ref, 0, cos_ref, sin_ref, rows_ref, block, slots_uv)
        row_tables(p, bins_ref, 1, cos_ref, sin_ref, cols_ref, block, slots_uv)
        flipped_tables(p, bins_ref, cos_ref, sin_ref, flip_ref, block, slots_uv)
        for at in range(0, size, CHUNK):
            cols = slice(at, at + CHUNK)
            gl = gx_ref[0, 0:1, cols]
            gr = gx_ref[2, 0:1, cols]
            gu = wide(gy_ref[0], CHUNK)
            gd = wide(gy_ref[2], CHUNK)
            left = gu * ul_ref[:, cols].astype(F32) + gd * dl_ref[:, cols].astype(F32)
            right = gu * ur_ref[:, cols].astype(F32) + gd * dr_ref[:, cols].astype(F32)
            beamed_ref[:size, cols] = (gl * left + gr * right).astype(BF16)
            low = gl * l_ref[:, cols].astype(F32) + gr * r_ref[:, cols].astype(F32)
            beamed_ref[size:, cols] = (wide(gy_ref[1], CHUNK) * low).astype(BF16)
        first_ref[:, size:] = early_ref[p]
        for at in range(0, size, CHUNK):
            cols = slice(at, at + CHUNK)
            first_ref[:, cols] = jnp.dot(
                rows_ref[...], beamed_ref[:, cols], preferred_element_type=F32
            ).astype(BF16)
        for k in range(slots_uv):
            rows = slice(k * pair, (k + 1) * pair)
            table = cols_ref[rows, :]
            both = lax.dot_general(
                first_ref[rows, :], table, (((1,), (1,)), ((), ())), preferred_element_type=F32
            )
            used = jnp.where(k < used_ref[p], 1.0, 0.0).astype(F32)
            weight = weight_ref[p, k].astype(F32) * used
            real = ((both[:block, :block] - both[block:, block:]) * weight).astype(BF16)
            turned = ((both[:block, block:] + both[block:, :block]) * weight).astype(BF16)
            scaled = jnp.concatenate(
                [
                    jnp.concatenate([real, turned], axis=1),
                    jnp.concatenate([turned, -real], axis=1),
                ],
                axis=0,
            )
            spread_ref[rows, :] = jnp.dot(scaled, table, preferred_element_type=F32).astype(BF16)
        late_ref[p] = spread_ref[:, size:]
        for at in range(0, size, CHUNK):
            cols = slice(at, at + CHUNK)
            gl = gx_ref[0, 0:1, cols]
            gr = gx_ref[2, 0:1, cols]
            top = jnp.dot(flip_ref[:size, :], spread_ref[:, cols], preferred_element_type=F32)
            up = wide(gy_ref[0], CHUNK) * top
            down = wide(gy_ref[2], CHUNK) * top
            acc_ref[0, :, cols] += gl * up
            acc_ref[2, :, cols] += gl * down
            acc_ref[3, :, cols] += gr * up
            acc_ref[5, :, cols] += gr * down
            low = jnp.dot(flip_ref[size:, :], spread_ref[:, cols], preferred_element_type=F32)
            low = wide(gy_ref[1], CHUNK) * low
            acc_ref[1, :, cols] += gl * low
            acc_ref[4, :, cols] += gr * low
        return carry

    lax.fori_loop(0, count_ref[0], step, 0)
    for part, out_ref in enumerate((oul_ref, ol_ref, odl_ref, our_ref, or_ref, odr_ref)):
        out_ref[...] = acc_ref[part].astype(BF16)


def late_kernel(
    count_ref, off_ref, bins_ref, decay_ref, cos_ref, sin_ref, late_ref,
    up_ref, own_ref, down_ref, gy_ref, gx_ref, flip_ref,
):
    size = own_ref.shape[0]
    block = flip_ref.shape[1] // bins_ref.shape[1]
    slots_uv = bins_ref.shape[1] // 2
    for out_ref in (up_ref, own_ref, down_ref):
        out_ref[...] = jnp.zeros_like(out_ref)

    def step(p, carry):
        beams(p, off_ref, decay_ref, gy_ref, gx_ref, size)
        flipped_tables(p, bins_ref, cos_ref, sin_ref, flip_ref, block, slots_uv)
        for at in range(0, size, CHUNK):
            cols = slice(at, at + CHUNK)
            gx = gx_ref[1, 0:1, cols]
            part = late_ref[p, :, cols]
            top = gx * jnp.dot(flip_ref[:size, :], part, preferred_element_type=F32)
            up_ref[:, cols] += wide(gy_ref[0], CHUNK) * top
            down_ref[:, cols] += wide(gy_ref[2], CHUNK) * top
            low = gx * jnp.dot(flip_ref[size:, :], part, preferred_element_type=F32)
            own_ref[:, cols] += wide(gy_ref[1], CHUNK) * low
        return carry

    lax.fori_loop(0, count_ref[0], step, 0)


def local_call(kernel, scalars, vectors, outs, scratch, flops):
    return pl.pallas_call(
        kernel,
        out_shape=outs,
        in_specs=[pl.BlockSpec(memory_space=pltpu.SMEM)] * len(scalars)
        + [pl.BlockSpec(memory_space=pltpu.VMEM)] * len(vectors),
        out_specs=jax.tree.map(lambda _: pl.BlockSpec(memory_space=pltpu.VMEM), outs),
        scratch_shapes=scratch,
        compiler_params=pltpu.CompilerParams(vmem_limit_bytes=56 * 1024 * 1024),
        cost_estimate=pl.CostEstimate(flops=flops, bytes_accessed=8 << 20, transcendentals=0),
    )(*scalars, *vectors)


def shards(sky, point_count, point_offset, beam_width, uv_bins, uv_count, uv_weight):
    size = sky.shape[0]
    length = 2 * size
    slots, slots_uv, block = uv_weight.shape[2], uv_weight.shape[3], uv_weight.shape[4]
    depth = 2 * slots_uv * block
    up = shifted(sky, "ty", 1)
    down = shifted(sky, "ty", -1)
    left = shifted(sky, "tx", 1)
    right = shifted(sky, "tx", -1)
    up_left = shifted(up, "tx", 1)
    up_right = shifted(up, "tx", -1)
    down_left = shifted(down, "tx", 1)
    down_right = shifted(down, "tx", -1)

    cos, sin = full_tables(length)
    count = point_count.reshape(1)
    offset = point_offset.reshape(slots, 2)
    bins = jnp.clip(uv_bins.reshape(slots, 2 * slots_uv), 0, length // block - 1)
    used = uv_count.reshape(slots)
    width = beam_width.reshape(slots).astype(F32)
    decay = 1.0 / (2.0 * width * width)
    weight = uv_weight.reshape(slots, slots_uv, block, block)

    gy = pltpu.VMEM((3, size, 128), F32)
    gx = pltpu.VMEM((3, 8, size), F32)
    rows = pltpu.VMEM((depth, length), BF16)
    flip = pltpu.VMEM((length, depth), BF16)
    beamed = pltpu.VMEM((length, size), BF16)
    half = jax.ShapeDtypeStruct((slots, depth, size), BF16)
    sent = jax.ShapeDtypeStruct((size, size), BF16)
    kept = jax.ShapeDtypeStruct((size, size), F32)
    flops = 2 * slots * depth * length * size

    early = local_call(
        early_kernel,
        (count, offset, bins, decay),
        (cos, sin, up, sky, down),
        half,
        [gy, gx, rows, beamed],
        flops,
    )
    to_ul, to_l, to_dl, to_ur, to_r, to_dr, late = local_call(
        middle_kernel,
        (count, offset, bins, used, decay),
        (cos, sin, weight, early, up_left, left, down_left, up_right, right, down_right),
        (sent,) * 6 + (half,),
        [
            gy, gx, rows, rows, flip, beamed,
            pltpu.VMEM((depth, length), BF16),
            pltpu.VMEM((depth, length), BF16),
            pltpu.VMEM((6, size, size), F32),
        ],
        3 * flops,
    )
    from_ul = shifted(to_ur, "tx", 1)
    from_ur = shifted(to_ul, "tx", -1)
    from_dl = shifted(to_dr, "tx", 1)
    from_dr = shifted(to_dl, "tx", -1)
    from_l = shifted(to_r, "tx", 1)
    from_r = shifted(to_l, "tx", -1)
    to_up, own, to_down = local_call(
        late_kernel,
        (count, offset, bins, decay),
        (cos, sin, late),
        (kept,) * 3,
        [gy, gx, flip],
        flops,
    )
    to_up = (to_up + from_ul.astype(F32) + from_ur.astype(F32)).astype(BF16)
    to_down = (to_down + from_dl.astype(F32) + from_dr.astype(F32)).astype(BF16)
    from_down = shifted(to_up, "ty", -1)
    from_up = shifted(to_down, "ty", 1)
    result = own + from_l.astype(F32) + from_r.astype(F32)
    return result + from_down.astype(F32) + from_up.astype(F32)


def solution(mesh):
    in_specs = (
        P("ty", "tx"),
        P("ty", "tx"),
        P("ty", "tx", None, None),
        P("ty", "tx", None),
        P("ty", "tx", None, None, None),
        P("ty", "tx", None),
        P("ty", "tx", None, None, None, None),
    )
    out_specs = P("ty", "tx")
    return jax.shard_map(shards, mesh=mesh, in_specs=in_specs, out_specs=out_specs, check_vma=False)
```

time: 417 us -> 126 us (0.30); the launches traced: 410 us -> 125 us
  local copies, waits for them, and re-layouts: 154 us -> 2.4 us
  other arithmetic: 93 us -> 21.6 us
  waiting for transfers between devices: 80.9 us -> 20.6 us
  starting transfers between devices: 26.8 us -> 53.1 us
  Pallas kernels: 0 us -> 26.1 us
  loops' own time: 23.1 us -> 0 us
  between operations: 17.3 us -> 0.98 us
  matrix products: 14.9 us -> 0 us
    dynamic_update_slice x4 -> x0, local copies, waits for them, and re-layouts: 97.6 us -> none  [add_patch(): lax.dynamic_update_slice(total, current + update, (offset[0], offset[1]))]
    ppermute x11 -> x0, waiting for transfers between devices: 43.5 us -> none  [the longest x2 25 us: padded(): lax.ppermute(lax.slice_in_dim(block, block.shape[dim] - width, None, axis...]
    ppermute x4 -> x16, starting transfers between devices: 12.7 us -> 53.1 us  [shifted(): lax.ppermute(value, axis, [(source, source + steps) for source in range(f...]
    pallas_call x0 -> x3, Pallas kernels: none -> 26.1 us  [local_call(): pl.pallas_call(kernel, out_shape=outs, in_specs=[pl.BlockSpec(memory_spac...]
    another operation x2 -> x0, loops' own time: 23.1 us -> none  [the longest x1 20.4 us: shards(): lax.map(lambda item: beam_window(item[0], item[1]), (offsets, widths))]
    gather x8 -> x0, local copies, waits for them, and re-layouts: 21.6 us -> none  [the longest x7 21.1 us: gather_pool(): jnp.take(jnp.concatenate([own_values, got_values], axis=0), pool_index, a...]
    add x8 -> x1, other arithmetic: 21.7 us -> 1.35 us  [shards(): return result + from_down.astype(F32) + from_up.astype(F32)]
    dynamic_update_slice x4 -> x0, other arithmetic: 19.7 us -> none  [shards(): lax.map(lambda item: beam_window(item[0], item[1]), (offsets, widths))]
  transfers between devices with their start and end apart: 15 -> 16, of which waited for: 10 -> 3; matrix products, arithmetic and copies ran while one was open for 19% -> 17% of each run, Pallas kernels for 0% -> 11%
where the time goes in v1:
time: 126 us; the launch traced here: 125 us
  starting transfers between devices  53.1 us (42%)
  Pallas kernels  26.1 us (21%)
  other arithmetic  21.6 us (17%)
  waiting for transfers between devices  20.6 us (16%)
  local copies, waits for them, and re-layouts  2.4 us (2%)
    ppermute x16, starting transfers between devices, shifted(): lax.ppermute(value, axis, [(source, source + steps) for source in range(f...  53.1 us
    pallas_call x3, Pallas kernels, local_call(): pl.pallas_call(kernel, out_shape=outs, in_specs=[pl.BlockSpec(memory_spac...  26.1 us
    ppermute x16, waiting for transfers between devices, shifted(): lax.ppermute(value, axis, [(source, source + steps) for source in range(f...  20.6 us
    convert_element_type x1, other arithmetic, full_tables(): (jnp.sin(angle) * factor).astype(BF16)  18 us
  transfers between devices with their start and end apart: 16, of which 3 were waited for; matrix products, arithmetic and copies ran while one was open for 17% of the time, Pallas kernels for 11%

profile of v1, /device:TPU:21, one launch (start us, length us, event | category | flops | bytes accessed | tf_op | source)
XLA Modules:
  0.0 124.9 jit_solution(15647006037140455992)
XLA Ops:
  0.0 0.0 copy-start.2
  0.0 0.0 copy-start.3
  0.0 3.2 %collective-permute-start.1 = (bf16[512,512]{1,0:T(8,128)(2,1)}, bf16[512,512]{1,0:T(8,128)(2,1)S(1)}, u32[]{:S(2)}, u32[]{:S(2)}) collective-permute-start(bf16[512,512]{1,0:T(8,128)(2,1)} %own_ref.1), channel_id=1, source_target_pairs={{8,0},{16,8},{24,16},{9,1},{17,9},{25,17},{10,2},{18,10},{26,18},{... | collective-permute-start | bytes 1572872 | tf_op jit(solution)/shard_map/ppermute | solution.py:19
  3.2 2.3 %collective-permute-start = (bf16[512,512]{1,0:T(8,128)(2,1)}, bf16[512,512]{1,0:T(8,128)(2,1)S(1)}, u32[]{:S(2)}, u32[]{:S(2)}) collective-permute-start(bf16[512,512]{1,0:T(8,128)(2,1)} %own_ref.1), channel_id=1, source_target_pairs={{0,8},{8,16},{16,24},{1,9},{9,17},{17,25},{2,10},{10,18},{18,26},{... | collective-permute-start | bytes 1572872 | tf_op jit(solution)/shard_map/ppermute | solution.py:19
  5.5 3.1 %collective-permute-start.6 = (bf16[512,512]{1,0:T(8,128)(2,1)}, bf16[512,512]{1,0:T(8,128)(2,1)S(1)}, u32[]{:S(2)}, u32[]{:S(2)}) collective-permute-start(bf16[512,512]{1,0:T(8,128)(2,1)} %own_ref.1), channel_id=1, source_target_pairs={{1,0},{2,1},{3,2},{4,3},{5,4},{6,5},{7,6},{9,8},{10,9},{11,10},{12... | collective-permute-start | bytes 1572872 | tf_op jit(solution)/shard_map/ppermute | solution.py:19
  8.6 3.1 %collective-permute-start.3 = (bf16[512,512]{1,0:T(8,128)(2,1)}, bf16[512,512]{1,0:T(8,128)(2,1)S(1)}, u32[]{:S(2)}, u32[]{:S(2)}) collective-permute-start(bf16[512,512]{1,0:T(8,128)(2,1)} %own_ref.1), channel_id=1, source_target_pairs={{0,1},{1,2},{2,3},{3,4},{4,5},{5,6},{6,7},{8,9},{9,10},{10,11},{11... | collective-permute-start | bytes 1572872 | tf_op jit(solution)/shard_map/ppermute | solution.py:19
  11.7 18.0 %multiply_convert_fusion = (bf16[1024,1024]{1,0:T(8,128)(2,1)}, bf16[1024,1024]{1,0:T(8,128)(2,1)}) fusion(), kind=kLoop, calls=%fused_computation.6 | loop fusion | flops 18874368 | bytes 4194304 | tf_op jit(solution)/shard_map/convert_element_type | solution.py:27
  29.7 0.0 collective-permute-done.1.down_ref
  29.7 0.0 copy-start.8
  29.7 1.9 %collective-permute-start.7 = (bf16[512,512]{1,0:T(8,128)(2,1)S(1)}, bf16[512,512]{1,0:T(8,128)(2,1)S(1)}, u32[]{:S(2)}, u32[]{:S(2)}) collective-permute-start(bf16[512,512]{1,0:T(8,128)(2,1)S(1)} %collective-permute-done.1.down_ref), channel_id=1, source_target_pairs={{1,0},{2,1},{3,2},{4,3},{5,4},{6,5},{7,6},{9,8},{10,9},{11,10},{12... | collective-permute-start | bytes 1572872 | tf_op jit(solution)/shard_map/ppermute | solution.py:19
  31.6 3.6 %collective-permute-start.4 = (bf16[512,512]{1,0:T(8,128)(2,1)S(1)}, bf16[512,512]{1,0:T(8,128)(2,1)S(1)}, u32[]{:S(2)}, u32[]{:S(2)}) collective-permute-start(bf16[512,512]{1,0:T(8,128)(2,1)S(1)} %collective-permute-done.1.down_ref), channel_id=1, source_target_pairs={{0,1},{1,2},{2,3},{3,4},{4,5},{5,6},{6,7},{8,9},{9,10},{10,11},{11... | collective-permute-start | bytes 1572872 | tf_op jit(solution)/shard_map/ppermute | solution.py:19
  35.3 0.0 collective-permute-done.up_ref
  35.3 0.0 copy-start.7
  35.3 1.9 %collective-permute-start.5 = (bf16[512,512]{1,0:T(8,128)(2,1)S(1)}, bf16[512,512]{1,0:T(8,128)(2,1)}, u32[]{:S(2)}, u32[]{:S(2)}) collective-permute-start(bf16[512,512]{1,0:T(8,128)(2,1)S(1)} %collective-permute-done.up_ref), channel_id=1, source_target_pairs={{1,0},{2,1},{3,2},{4,3},{5,4},{6,5},{7,6},{9,8},{10,9},{11,10},{12... | collective-permute-start | bytes 1572872 | tf_op jit(solution)/shard_map/ppermute | solution.py:19
  37.2 0.0 collective-permute-done.6.r_ref
  37.2 0.0 copy-start.5
  37.3 3.6 %collective-permute-start.2 = (bf16[512,512]{1,0:T(8,128)(2,1)S(1)}, bf16[512,512]{1,0:T(8,128)(2,1)}, u32[]{:S(2)}, u32[]{:S(2)}) collective-permute-start(bf16[512,512]{1,0:T(8,128)(2,1)S(1)} %collective-permute-done.up_ref), channel_id=1, source_target_pairs={{0,1},{1,2},{2,3},{3,4},{4,5},{5,6},{6,7},{8,9},{9,10},{10,11},{11... | collective-permute-start | bytes 1572872 | tf_op jit(solution)/shard_map/ppermute | solution.py:19
  40.9 0.0 copy-done.2
  41.6 0.0 copy-done.3
  41.6 0.6 copy.12.off_ref
  42.2 0.7 copy.13.bins_ref
  42.9 0.0 copy-done.11
  42.9 0.5 fusion.6.decay_ref
  43.4 0.0 copy-done.8
  43.4 0.0 copy-done.7
  43.4 6.2 %shard_map.73.early_ref = bf16[4,512,512]{2,1,0:T(8,128)(2,1)} custom-call(s32[1]{0:T(128)} %bitcast.8.count_ref, s32[4,2]{1,0:T(4,128)} %copy.12.off_ref, s32[4,4]{1,0:T(4,128)} %copy.13.bins_ref, f32[4]{0:T(128)} %fusion.6.decay_ref, bf16[1024,1024]{1,0:T(8,128)(2,1)} %get-tuple-element.26.cos_ref, bf16[1024,1024]{1,0:T(8,128)(2,1)} %get-tuple-element.25.sin_ref, ...), custom_call_target="tpu_custom_call" | custom-call | flops 2147483648 | bytes 8388608 | tf_op jit(solution)/shard_map/pallas_call | solution.py:202
  49.6 0.0 copy-done.5
  49.6 0.0 collective-permute-done.3.l_ref
  49.7 0.0 copy-start.6
  49.7 0.0 collective-permute-done.7.dr_ref
  49.7 0.0 copy-start.9
  49.7 0.0 collective-permute-done.4.dl_ref
  49.7 0.0 copy-start.10
  49.7 0.0 collective-permute-done.5.ur_ref
  49.7 0.0 collective-permute-done.2.ul_ref
  49.7 0.7 copy-done.6
  50.4 0.2 copy-done.9
  50.6 0.2 copy-done.10
  50.8 12.9 %shard_map.74 = (bf16[512,512]{1,0:T(8,128)(2,1)}, bf16[512,512]{1,0:T(8,128)(2,1)}, bf16[512,512]{1,0:T(8,128)(2,1)}, bf16[512,512]{1,0:T(8,128)(2,1)}, bf16[51...) custom-call(s32[1]{0:T(128)} %bitcast.9.count_ref, s32[4,2]{1,0:T(4,128)} %copy.12.off_ref, ...), custom_call_target="tpu_custom_call" | custom-call | flops 6442450944 | bytes 8388608 | tf_op jit(solution)/shard_map/pallas_call | solution.py:202
  63.7 10.4 %collective-permute-start.10 = (bf16[512,512]{1,0:T(8,128)(2,1)}, bf16[512,512]{1,0:T(8,128)(2,1)S(1)}, u32[]{:S(2)}, u32[]{:S(2)}) collective-permute-start(bf16[512,512]{1,0:T(8,128)(2,1)} %get-tuple-element.20), channel_id=1, source_target_pairs={{0,1},{1,2},{2,3},{3,4},{4,5},{5,6},{6,7},{8,9},{9,10},{10,11},{11... | collective-permute-start | bytes 1572872 | tf_op jit(solution)/shard_map/ppermute | solution.py:19
  74.1 1.9 %collective-permute-start.11 = (bf16[512,512]{1,0:T(8,128)(2,1)}, bf16[512,512]{1,0:T(8,128)(2,1)S(1)}, u32[]{:S(2)}, u32[]{:S(2)}) collective-permute-start(bf16[512,512]{1,0:T(8,128)(2,1)} %get-tuple-element.21), channel_id=1, source_target_pairs={{1,0},{2,1},{3,2},{4,3},{5,4},{6,5},{7,6},{9,8},{10,9},{11,10},{12... | collective-permute-start | bytes 1572872 | tf_op jit(solution)/shard_map/ppermute | solution.py:19
  76.0 3.6 %collective-permute-start.13 = (bf16[512,512]{1,0:T(8,128)(2,1)}, bf16[512,512]{1,0:T(8,128)(2,1)S(1)}, u32[]{:S(2)}, u32[]{:S(2)}) collective-permute-start(bf16[512,512]{1,0:T(8,128)(2,1)} %get-tuple-element.23), channel_id=1, source_target_pairs={{0,1},{1,2},{2,3},{3,4},{4,5},{5,6},{6,7},{8,9},{9,10},{10,11},{11... | collective-permute-start | bytes 1572872 | tf_op jit(solution)/shard_map/ppermute | solution.py:19
  79.7 1.9 %collective-permute-start.14 = (bf16[512,512]{1,0:T(8,128)(2,1)}, bf16[512,512]{1,0:T(8,128)(2,1)S(1)}, u32[]{:S(2)}, u32[]{:S(2)}) collective-permute-start(bf16[512,512]{1,0:T(8,128)(2,1)} %get-tuple-element.24), channel_id=1, source_target_pairs={{1,0},{2,1},{3,2},{4,3},{5,4},{6,5},{7,6},{9,8},{10,9},{11,10},{12... | collective-permute-start | bytes 1572872 | tf_op jit(solution)/shard_map/ppermute | solution.py:19
  81.6 3.6 %collective-permute-start.8 = (bf16[512,512]{1,0:T(8,128)(2,1)}, bf16[512,512]{1,0:T(8,128)(2,1)S(1)}, u32[]{:S(2)}, u32[]{:S(2)}) collective-permute-start(bf16[512,512]{1,0:T(8,128)(2,1)} %get-tuple-element.17), channel_id=1, source_target_pairs={{0,1},{1,2},{2,3},{3,4},{4,5},{5,6},{6,7},{8,9},{9,10},{10,11},{11... | collective-permute-start | bytes 1572872 | tf_op jit(solution)/shard_map/ppermute | solution.py:19
  85.2 0.0 copy-start.4
  85.2 7.0 %shard_map.75 = (f32[512,512]{1,0:T(8,128)}, f32[512,512]{1,0:T(8,128)}, f32[512,512]{1,0:T(8,128)}) custom-call(s32[1]{0:T(128)} %bitcast.10.count_ref, s32[4,2]{1,0:T(4,128)} %copy.12.off_ref, s32[4,4]{1,0:T(4,128)} %copy.13.bins_ref, f32[4]{0:T(128)} %fusion.6.decay_ref, bf16[1024,1024]{1,0:T(8,128)(2,1)} %get-tuple-element.26.cos_ref, ...), custom_call_target="tpu_custom_call" | custom-call | flops 2147483648 | bytes 8388608 | tf_op jit(solution)/shard_map/pallas_call | solution.py:202
  92.2 0.0 collective-permute-done.10
  92.3 0.0 copy-done.4
  92.3 2.1 %collective-permute-start.9 = (bf16[512,512]{1,0:T(8,128)(2,1)S(1)}, bf16[512,512]{1,0:T(8,128)(2,1)S(1)}, u32[]{:S(2)}, u32[]{:S(2)}) collective-permute-start(bf16[512,512]{1,0:T(8,128)(2,1)S(1)} %copy-done.4), channel_id=1, source_target_pairs={{1,0},{2,1},{3,2},{4,3},{5,4},{6,5},{7,6},{9,8},{10,9},{11,10},{12... | collective-permute-start | bytes 1572872 | tf_op jit(solution)/shard_map/ppermute | solution.py:19
  94.3 0.0 collective-permute-done.11
  94.3 0.0 copy-start.1
  94.3 1.5 %add_convert_fusion.1 = bf16[512,512]{1,0:T(8,128)(2,1)S(1)} fusion(bf16[512,512]{1,0:T(8,128)(2,1)S(1)} %collective-permute-done.11, f32[512,512]{1,0:T(8,128)} %get-tuple-element.19, bf16[512,512]{1,0:T(8,128)(2,1)S(1)} %collective-permute-done.10), kind=kLoop, calls=%fused_computation.13 | loop fusion | flops 1310720 | bytes 2621440 | tf_op jit(solution)/shard_map/convert_element_type | solution.py:282
  95.9 4.8 %collective-permute-start.12 = (bf16[512,512]{1,0:T(8,128)(2,1)S(1)}, bf16[512,512]{1,0:T(8,128)(2,1)S(1)}, u32[]{:S(2)}, u32[]{:S(2)}) collective-permute-start(bf16[512,512]{1,0:T(8,128)(2,1)S(1)} %add_convert_fusion.1), channel_id=1, source_target_pairs={{8,0},{16,8},{24,16},{9,1},{17,9},{25,17},{10,2},{18,10},{26,18},{... | collective-permute-start | bytes 1572872 | tf_op jit(solution)/shard_map/ppermute | solution.py:19
  100.7 0.0 collective-permute-done.13
  100.7 0.0 collective-permute-done.14
  100.7 0.0 copy-done
  100.7 0.2 add_convert_fusion
  101.0 1.9 %collective-permute-start.15 = (bf16[512,512]{1,0:T(8,128)(2,1)S(1)}, bf16[512,512]{1,0:T(8,128)(2,1)S(1)}, u32[]{:S(2)}, u32[]{:S(2)}) collective-permute-start(bf16[512,512]{1,0:T(8,128)(2,1)S(1)} %add_convert_fusion), channel_id=1, source_target_pairs={{0,8},{8,16},{16,24},{1,9},{9,17},{17,25},{2,10},{10,18},{18,26},{... | collective-permute-start | bytes 1572872 | tf_op jit(solution)/shard_map/ppermute | solution.py:19
  102.9 0.0 collective-permute-done.8
  102.9 0.6 collective-permute-done.9
  103.5 7.7 %collective-permute-done.12 = bf16[512,512]{1,0:T(8,128)(2,1)S(1)} collective-permute-done((bf16[512,512]{1,0:T(8,128)(2,1)S(1)}, bf16[512,512]{1,0:T(8,128)(2,1)S(1)}, u32[]{:S(2)}, u32[]{:S(2)}) %collective-permute-start.12) | collective-permute-done | bytes 524320 | tf_op jit(solution)/shard_map/ppermute | solution.py:19
  111.3 12.3 %collective-permute-done.15 = bf16[512,512]{1,0:T(8,128)(2,1)S(1)} collective-permute-done((bf16[512,512]{1,0:T(8,128)(2,1)S(1)}, bf16[512,512]{1,0:T(8,128)(2,1)S(1)}, u32[]{:S(2)}, u32[]{:S(2)}) %collective-permute-start.15) | collective-permute-done | bytes 524320 | tf_op jit(solution)/shard_map/ppermute | solution.py:19
  123.5 0.0 copy-done.1
  123.5 1.4 %convert_add_fusion = f32[512,512]{1,0:T(8,128)} fusion(bf16[512,512]{1,0:T(8,128)(2,1)S(1)} %collective-permute-done.15, bf16[512,512]{1,0:T(8,128)(2,1)S(1)} %collective-permute-done.12, bf16[512,512]{1,0:T(8,128)(2,1)S(1)} %collective-permute-done.9, f32[512,512]{1,0:T(8,128)S(1)} %copy-done.1, bf16[512,512]{1,0:T(8,128)(2,1)S(1)} %collective-permute-done.8), kind=kLoop, calls=%fused_computation.11 | loop fusion | flops 2097152 | bytes 4194304 | tf_op jit(solution)/shard_map/add | solution.py:287
  (3 shorter events, 0.0 us)
Async XLA Ops:
  0.0 40.9 %copy-start.2 = (s32[1,1,4,2,2]{2,4,3,1,0:T(2,128)S(1)}, s32[1,1,4,2,2]{2,4,3,1,0:T(2,128)}, u32[]{:S(2)}) copy-start(s32[1,1,4,2,2]{2,4,3,1,0:T(2,128)} %param.11) | copy-start | bytes 196
  0.0 41.6 %copy-start.3 = (s32[1,1,4,2]{2,3,1,0:T(2,128)S(1)}, s32[1,1,4,2]{2,3,1,0:T(2,128)}, u32[]{:S(2)}) copy-start(s32[1,1,4,2]{2,3,1,0:T(2,128)} %param.9) | copy-start | bytes 100
  0.0 42.9 %copy-start.11 = (bf16[1,1,4]{2,1,0:T(2,128)(2,1)S(1)}, bf16[1,1,4]{2,1,0:T(2,128)(2,1)}, u32[]{:S(2)}) copy-start(bf16[1,1,4]{2,1,0:T(2,128)(2,1)} %param.10) | copy-start | bytes 28
  0.0 29.7 %collective-permute-start.1 = (bf16[512,512]{1,0:T(8,128)(2,1)}, bf16[512,512]{1,0:T(8,128)(2,1)S(1)}, u32[]{:S(2)}, u32[]{:S(2)}) collective-permute-start(bf16[512,512]{1,0:T(8,128)(2,1)} %own_ref.1), channel_id=1, source_target_pairs={{8,0},{16,8},{24,16},{9,1},{17,9},{25,17},{10,2},{18,10},{26,18},{... | collective-permute-start | bytes 1572872 | tf_op jit(solution)/shard_map/ppermute | solution.py:19
  3.2 32.1 %collective-permute-start = (bf16[512,512]{1,0:T(8,128)(2,1)}, bf16[512,512]{1,0:T(8,128)(2,1)S(1)}, u32[]{:S(2)}, u32[]{:S(2)}) collective-permute-start(bf16[512,512]{1,0:T(8,128)(2,1)} %own_ref.1), channel_id=1, source_target_pairs={{0,8},{8,16},{16,24},{1,9},{9,17},{17,25},{2,10},{10,18},{18,26},{... | collective-permute-start | bytes 1572872 | tf_op jit(solution)/shard_map/ppermute | solution.py:19
  5.5 31.8 %collective-permute-start.6 = (bf16[512,512]{1,0:T(8,128)(2,1)}, bf16[512,512]{1,0:T(8,128)(2,1)S(1)}, u32[]{:S(2)}, u32[]{:S(2)}) collective-permute-start(bf16[512,512]{1,0:T(8,128)(2,1)} %own_ref.1), channel_id=1, source_target_pairs={{1,0},{2,1},{3,2},{4,3},{5,4},{6,5},{7,6},{9,8},{10,9},{11,10},{12... | collective-permute-start | bytes 1572872 | tf_op jit(solution)/shard_map/ppermute | solution.py:19
  8.6 41.0 %collective-permute-start.3 = (bf16[512,512]{1,0:T(8,128)(2,1)}, bf16[512,512]{1,0:T(8,128)(2,1)S(1)}, u32[]{:S(2)}, u32[]{:S(2)}) collective-permute-start(bf16[512,512]{1,0:T(8,128)(2,1)} %own_ref.1), channel_id=1, source_target_pairs={{0,1},{1,2},{2,3},{3,4},{4,5},{5,6},{6,7},{8,9},{9,10},{10,11},{11... | collective-permute-start | bytes 1572872 | tf_op jit(solution)/shard_map/ppermute | solution.py:19
  29.7 13.7 %copy-start.8 = (bf16[512,512]{1,0:T(8,128)(2,1)}, bf16[512,512]{1,0:T(8,128)(2,1)S(1)}, u32[]{:S(2)}) copy-start(bf16[512,512]{1,0:T(8,128)(2,1)S(1)} %collective-permute-done.1.down_ref) | copy-start | bytes 1572868
  29.7 20.0 %collective-permute-start.7 = (bf16[512,512]{1,0:T(8,128)(2,1)S(1)}, bf16[512,512]{1,0:T(8,128)(2,1)S(1)}, u32[]{:S(2)}, u32[]{:S(2)}) collective-permute-start(bf16[512,512]{1,0:T(8,128)(2,1)S(1)} %collective-permute-done.1.down_ref), channel_id=1, source_target_pairs={{1,0},{2,1},{3,2},{4,3},{5,4},{6,5},{7,6},{9,8},{10,9},{11,10},{12... | collective-permute-start | bytes 1572872 | tf_op jit(solution)/shard_map/ppermute | solution.py:19
  31.6 18.1 %collective-permute-start.4 = (bf16[512,512]{1,0:T(8,128)(2,1)S(1)}, bf16[512,512]{1,0:T(8,128)(2,1)S(1)}, u32[]{:S(2)}, u32[]{:S(2)}) collective-permute-start(bf16[512,512]{1,0:T(8,128)(2,1)S(1)} %collective-permute-done.1.down_ref), channel_id=1, source_target_pairs={{0,1},{1,2},{2,3},{3,4},{4,5},{5,6},{6,7},{8,9},{9,10},{10,11},{11... | collective-permute-start | bytes 1572872 | tf_op jit(solution)/shard_map/ppermute | solution.py:19
  35.3 8.1 %copy-start.7 = (bf16[512,512]{1,0:T(8,128)(2,1)}, bf16[512,512]{1,0:T(8,128)(2,1)S(1)}, u32[]{:S(2)}) copy-start(bf16[512,512]{1,0:T(8,128)(2,1)S(1)} %collective-permute-done.up_ref) | copy-start | bytes 1572868
  35.3 14.4 %collective-permute-start.5 = (bf16[512,512]{1,0:T(8,128)(2,1)S(1)}, bf16[512,512]{1,0:T(8,128)(2,1)}, u32[]{:S(2)}, u32[]{:S(2)}) collective-permute-start(bf16[512,512]{1,0:T(8,128)(2,1)S(1)} %collective-permute-done.up_ref), channel_id=1, source_target_pairs={{1,0},{2,1},{3,2},{4,3},{5,4},{6,5},{7,6},{9,8},{10,9},{11,10},{12... | collective-permute-start | bytes 1572872 | tf_op jit(solution)/shard_map/ppermute | solution.py:19
  37.2 12.4 %copy-start.5 = (bf16[512,512]{1,0:T(8,128)(2,1)}, bf16[512,512]{1,0:T(8,128)(2,1)S(1)}, u32[]{:S(2)}) copy-start(bf16[512,512]{1,0:T(8,128)(2,1)S(1)} %collective-permute-done.6.r_ref) | copy-start | bytes 1572868
  37.3 12.5 %collective-permute-start.2 = (bf16[512,512]{1,0:T(8,128)(2,1)S(1)}, bf16[512,512]{1,0:T(8,128)(2,1)}, u32[]{:S(2)}, u32[]{:S(2)}) collective-permute-start(bf16[512,512]{1,0:T(8,128)(2,1)S(1)} %collective-permute-done.up_ref), channel_id=1, source_target_pairs={{0,1},{1,2},{2,3},{3,4},{4,5},{5,6},{6,7},{8,9},{9,10},{10,11},{11... | collective-permute-start | bytes 1572872 | tf_op jit(solution)/shard_map/ppermute | solution.py:19
  49.7 0.8 copy-start.6
  49.7 0.9 copy-start.9
  49.7 1.1 copy-start.10
  63.7 28.6 %collective-permute-start.10 = (bf16[512,512]{1,0:T(8,128)(2,1)}, bf16[512,512]{1,0:T(8,128)(2,1)S(1)}, u32[]{:S(2)}, u32[]{:S(2)}) collective-permute-start(bf16[512,512]{1,0:T(8,128)(2,1)} %get-tuple-element.20), channel_id=1, source_target_pairs={{0,1},{1,2},{2,3},{3,4},{4,5},{5,6},{6,7},{8,9},{9,10},{10,11},{11... | collective-permute-start | bytes 1572872 | tf_op jit(solution)/shard_map/ppermute | solution.py:19
  74.1 20.2 %collective-permute-start.11 = (bf16[512,512]{1,0:T(8,128)(2,1)}, bf16[512,512]{1,0:T(8,128)(2,1)S(1)}, u32[]{:S(2)}, u32[]{:S(2)}) collective-permute-start(bf16[512,512]{1,0:T(8,128)(2,1)} %get-tuple-element.21), channel_id=1, source_target_pairs={{1,0},{2,1},{3,2},{4,3},{5,4},{6,5},{7,6},{9,8},{10,9},{11,10},{12... | collective-permute-start | bytes 1572872 | tf_op jit(solution)/shard_map/ppermute | solution.py:19
  76.0 24.7 %collective-permute-start.13 = (bf16[512,512]{1,0:T(8,128)(2,1)}, bf16[512,512]{1,0:T(8,128)(2,1)S(1)}, u32[]{:S(2)}, u32[]{:S(2)}) collective-permute-start(bf16[512,512]{1,0:T(8,128)(2,1)} %get-tuple-element.23), channel_id=1, source_target_pairs={{0,1},{1,2},{2,3},{3,4},{4,5},{5,6},{6,7},{8,9},{9,10},{10,11},{11... | collective-permute-start | bytes 1572872 | tf_op jit(solution)/shard_map/ppermute | solution.py:19
  79.7 21.1 %collective-permute-start.14 = (bf16[512,512]{1,0:T(8,128)(2,1)}, bf16[512,512]{1,0:T(8,128)(2,1)S(1)}, u32[]{:S(2)}, u32[]{:S(2)}) collective-permute-start(bf16[512,512]{1,0:T(8,128)(2,1)} %get-tuple-element.24), channel_id=1, source_target_pairs={{1,0},{2,1},{3,2},{4,3},{5,4},{6,5},{7,6},{9,8},{10,9},{11,10},{12... | collective-permute-start | bytes 1572872 | tf_op jit(solution)/shard_map/ppermute | solution.py:19
  81.6 21.3 %collective-permute-start.8 = (bf16[512,512]{1,0:T(8,128)(2,1)}, bf16[512,512]{1,0:T(8,128)(2,1)S(1)}, u32[]{:S(2)}, u32[]{:S(2)}) collective-permute-start(bf16[512,512]{1,0:T(8,128)(2,1)} %get-tuple-element.17), channel_id=1, source_target_pairs={{0,1},{1,2},{2,3},{3,4},{4,5},{5,6},{6,7},{8,9},{9,10},{10,11},{11... | collective-permute-start | bytes 1572872 | tf_op jit(solution)/shard_map/ppermute | solution.py:19
  85.2 7.0 %copy-start.4 = (bf16[512,512]{1,0:T(8,128)(2,1)S(1)}, bf16[512,512]{1,0:T(8,128)(2,1)}, u32[]{:S(2)}) copy-start(bf16[512,512]{1,0:T(8,128)(2,1)} %get-tuple-element.18) | copy-start | bytes 1572868
  92.2 8.5 %copy-start = (f32[512,512]{1,0:T(8,128)S(1)}, f32[512,512]{1,0:T(8,128)}, u32[]{:S(2)}) copy-start(f32[512,512]{1,0:T(8,128)} %get-tuple-element.22) | copy-start | bytes 3145732
  92.3 11.3 %collective-permute-start.9 = (bf16[512,512]{1,0:T(8,128)(2,1)S(1)}, bf16[512,512]{1,0:T(8,128)(2,1)S(1)}, u32[]{:S(2)}, u32[]{:S(2)}) collective-permute-start(bf16[512,512]{1,0:T(8,128)(2,1)S(1)} %copy-done.4), channel_id=1, source_target_pairs={{1,0},{2,1},{3,2},{4,3},{5,4},{6,5},{7,6},{9,8},{10,9},{11,10},{12... | collective-permute-start | bytes 1572872 | tf_op jit(solution)/shard_map/ppermute | solution.py:19
  94.3 29.2 %copy-start.1 = (f32[512,512]{1,0:T(8,128)S(1)}, f32[512,512]{1,0:T(8,128)}, u32[]{:S(2)}) copy-start(f32[512,512]{1,0:T(8,128)} %get-tuple-element.16) | copy-start | bytes 3145732
  95.9 15.4 %collective-permute-start.12 = (bf16[512,512]{1,0:T(8,128)(2,1)S(1)}, bf16[512,512]{1,0:T(8,128)(2,1)S(1)}, u32[]{:S(2)}, u32[]{:S(2)}) collective-permute-start(bf16[512,512]{1,0:T(8,128)(2,1)S(1)} %add_convert_fusion.1), channel_id=1, source_target_pairs={{8,0},{16,8},{24,16},{9,1},{17,9},{25,17},{10,2},{18,10},{26,18},{... | collective-permute-start | bytes 1572872 | tf_op jit(solution)/shard_map/ppermute | solution.py:19
  101.0 22.5 %collective-permute-start.15 = (bf16[512,512]{1,0:T(8,128)(2,1)S(1)}, bf16[512,512]{1,0:T(8,128)(2,1)S(1)}, u32[]{:S(2)}, u32[]{:S(2)}) collective-permute-start(bf16[512,512]{1,0:T(8,128)(2,1)S(1)} %add_convert_fusion), channel_id=1, source_target_pairs={{0,8},{8,16},{16,24},{1,9},{9,17},{17,25},{2,10},{10,18},{18,26},{... | collective-permute-start | bytes 1572872 | tf_op jit(solution)/shard_map/ppermute | solution.py:19

commit v2 on v1

--- a/solution.py
+++ b/solution.py
@@ -11,20 +11,20 @@
 F32 = jnp.float32
 BF16 = jnp.bfloat16
 CHUNK = 256
-
-
-def shifted(value, axis, steps):
-    count = lax.axis_size(axis)
-    first, last = (max(0, -steps), min(count, count - steps))
-    return lax.ppermute(value, axis, [(source, source + steps) for source in range(first, last)])
-
-
-def full_tables(length):
-    index = jnp.arange(length, dtype=jnp.int32)
-    phase = index[:, None] * index[None, :] % length
+BANDS = 2
+FINE = 32
+MESH = pl.DeviceIdType.MESH
+
+
+def small_tables(length, fine):
+    pixels = jnp.arange(length, dtype=jnp.int32)
+    rows = jnp.concatenate(
+        [jnp.arange(fine, dtype=jnp.int32), fine * jnp.arange(length // fine, dtype=jnp.int32)]
+    )
+    phase = rows[:, None] * pixels[None, :] % length
     angle = phase.astype(F32) * (2.0 * math.pi / length)
-    factor = 1.0 / math.sqrt(length)
-    return (jnp.cos(angle) * factor).astype(BF16), (jnp.sin(angle) * factor).astype(BF16)
+    scale = jnp.where(jnp.arange(rows.shape[0]) < fine, 1.0 / math.sqrt(length), 1.0)[:, None]
+    return jnp.cos(angle) * scale, jnp.sin(angle) * scale
 
 
 def gaussians(start, decay, size, axis):
@@ -65,6 +65,154 @@
         at = pl.ds(pl.multiple_of(bins_ref[p, 2 * k] * block, block), block)
         flip_ref[:, (2 * k) * block : (2 * k + 1) * block] = cos_ref[:, at]
         flip_ref[:, (2 * k + 1) * block : (2 * k + 2) * block] = sin_ref[:, at]
+
+
+class Around:
+    def __init__(self):
+        ty, tx = lax.axis_index("ty"), lax.axis_index("tx")
+        ny, nx = lax.axis_size("ty"), lax.axis_size("tx")
+        self.has = (ty > 0, ty < ny - 1, tx > 0, tx < nx - 1)
+        self.to = ({"ty": ty - 1}, {"ty": ty + 1}, {"tx": tx - 1}, {"tx": tx + 1})
+
+    def greet(self):
+        barrier = pltpu.get_barrier_semaphore()
+        for side in range(4):
+
+            @pl.when(self.has[side])
+            def _(side=side):
+                pl.semaphore_signal(barrier, inc=1, device_id=self.to[side], device_id_type=MESH)
+
+        pl.semaphore_wait(barrier, sum(has.astype(jnp.int32) for has in self.has))
+
+
+UP, DOWN, LEFT, RIGHT = 0, 1, 2, 3
+BACK = (DOWN, UP, RIGHT, LEFT)
+
+
+def bands(size):
+    step = size // BANDS
+    return [slice(i * step, (i + 1) * step) for i in range(BANDS)]
+
+
+def halo_kernel(
+    cosines_ref, sines_ref, own_ref,
+    ul_ref, l_ref, dl_ref, ur_ref, r_ref, dr_ref, cos_out, sin_out, up_ref, down_ref,
+    zero_ref, cos_ref, sin_ref, y_send, y_recv, x_send, x_recv, out_sems, zero_sem,
+):
+    size = own_ref.shape[0]
+    length = 2 * size
+    fine = FINE
+    around = Around()
+    pieces = bands(size)
+    landing = {LEFT: (ur_ref, r_ref, dr_ref), RIGHT: (ul_ref, l_ref, dl_ref)}
+
+    def vertical(side, i):
+        target = down_ref if side == UP else up_ref
+        return pltpu.make_async_remote_copy(
+            src_ref=own_ref.at[pieces[i]],
+            dst_ref=target.at[pieces[i]],
+            send_sem=y_send.at[side, i],
+            recv_sem=y_recv.at[side, i],
+            device_id=around.to[side],
+            device_id_type=MESH,
+        )
+
+    def beside(side):
+        return pltpu.make_async_remote_copy(
+            src_ref=own_ref,
+            dst_ref=landing[side][1],
+            send_sem=x_send.at[side - LEFT, 2 * BANDS],
+            recv_sem=x_recv.at[side - LEFT, 2 * BANDS],
+            device_id=around.to[side],
+            device_id_type=MESH,
+        )
+
+    def corner(side, which, i):
+        source = up_ref if which == 0 else down_ref
+        return pltpu.make_async_remote_copy(
+            src_ref=source.at[pieces[i]],
+            dst_ref=landing[side][2 * which].at[pieces[i]],
+            send_sem=x_send.at[side - LEFT, which * BANDS + i],
+            recv_sem=x_recv.at[side - LEFT, which * BANDS + i],
+            device_id=around.to[side],
+            device_id_type=MESH,
+        )
+
+    zero_ref[...] = jnp.zeros_like(zero_ref)
+    around.greet()
+    for i in range(BANDS):
+        for side in (UP, DOWN):
+
+            @pl.when(around.has[side])
+            def _(side=side, i=i):
+                vertical(side, i).start()
+
+    for side in (LEFT, RIGHT):
+
+        @pl.when(around.has[side])
+        def _(side=side):
+            beside(side).start()
+
+        @pl.when(jnp.logical_not(around.has[side]))
+        def _(side=side):
+            for target in landing[BACK[side]]:
+                fill = pltpu.make_async_copy(zero_ref, target, zero_sem)
+                fill.start()
+                fill.wait()
+
+    for side, target in ((UP, up_ref), (DOWN, down_ref)):
+
+        @pl.when(jnp.logical_not(around.has[side]))
+        def _(target=target):
+            target[...] = jnp.zeros_like(target)
+
+    def table(j, carry):
+        c, s = cosines_ref[pl.ds(fine + j, 1), :], sines_ref[pl.ds(fine + j, 1), :]
+        fc, fs = cosines_ref[:fine, :], sines_ref[:fine, :]
+        at = pl.ds(pl.multiple_of(j * fine, fine), fine)
+        cos_ref[at, :] = (fc * c - fs * s).astype(BF16)
+        sin_ref[at, :] = (fs * c + fc * s).astype(BF16)
+        return carry
+
+    lax.fori_loop(0, length // fine, table, 0)
+
+    for i in range(BANDS):
+        for which, side in ((0, UP), (1, DOWN)):
+
+            @pl.when(around.has[side])
+            def _(side=side, i=i):
+                vertical(BACK[side], i).wait_recv()
+
+            for beyond in (LEFT, RIGHT):
+
+                @pl.when(around.has[beyond])
+                def _(beyond=beyond, which=which, i=i):
+                    corner(beyond, which, i).start()
+
+    cos_copy = pltpu.make_async_copy(cos_ref, cos_out, out_sems.at[0])
+    sin_copy = pltpu.make_async_copy(sin_ref, sin_out, out_sems.at[1])
+    cos_copy.start()
+    sin_copy.start()
+    for side in (UP, DOWN):
+
+        @pl.when(around.has[side])
+        def _(side=side):
+            for i in range(BANDS):
+                vertical(side, i).wait_send()
+
+    for side in (LEFT, RIGHT):
+
+        @pl.when(around.has[side])
+        def _(side=side):
+            beside(side).wait_send()
+            beside(BACK[side]).wait_recv()
+            for which in range(2):
+                for i in range(BANDS):
+                    corner(side, which, i).wait_send()
+                    corner(BACK[side], which, i).wait_recv()
+
+    cos_copy.wait()
+    sin_copy.wait()
 
 
 def early_kernel(
@@ -166,7 +314,12 @@
             acc_ref[4, :, cols] += gr * low
         return carry
 
+    def idle(p, carry):
+        late_ref[p] = jnp.zeros(late_ref.shape[1:], BF16)
+        return carry
+
     lax.fori_loop(0, count_ref[0], step, 0)
+    lax.fori_loop(count_ref[0], late_ref.shape[0], idle, 0)
     for part, out_ref in enumerate((oul_ref, ol_ref, odl_ref, our_ref, or_ref, odr_ref)):
         out_ref[...] = acc_ref[part].astype(BF16)
 
@@ -198,6 +351,130 @@
     lax.fori_loop(0, count_ref[0], step, 0)
 
 
+def sum_kernel(
+    ul_ref, l_ref, dl_ref, ur_ref, r_ref, dr_ref, up_ref, mid_ref, down_ref,
+    own_ref, above_ref, below_ref, got_ref, going_ref,
+    y_send, y_recv, x_send, x_recv,
+):
+    size = own_ref.shape[0]
+    around = Around()
+    pieces = bands(size)
+    leaving = {LEFT: (ul_ref, l_ref, dl_ref), RIGHT: (ur_ref, r_ref, dr_ref)}
+
+    def corner(side, which, i):
+        return pltpu.make_async_remote_copy(
+            src_ref=leaving[side][2 * which].at[pieces[i]],
+            dst_ref=got_ref.at[side - LEFT, 2 * which, pieces[i]],
+            send_sem=x_send.at[side - LEFT, which * BANDS + i],
+            recv_sem=x_recv.at[side - LEFT, which * BANDS + i],
+            device_id=around.to[side],
+            device_id_type=MESH,
+        )
+
+    def beside(side):
+        return pltpu.make_async_remote_copy(
+            src_ref=leaving[side][1],
+            dst_ref=got_ref.at[side - LEFT, 1],
+            send_sem=x_send.at[side - LEFT, 2 * BANDS],
+            recv_sem=x_recv.at[side - LEFT, 2 * BANDS],
+            device_id=around.to[side],
+            device_id_type=MESH,
+        )
+
+    def vertical(side, i):
+        target = below_ref if side == UP else above_ref
+        return pltpu.make_async_remote_copy(
+            src_ref=going_ref.at[side, pieces[i]],
+            dst_ref=target.at[pieces[i]],
+            send_sem=y_send.at[side, i],
+            recv_sem=y_recv.at[side, i],
+            device_id=around.to[side],
+            device_id_type=MESH,
+        )
+
+    around.greet()
+    for i in range(BANDS):
+        for which in range(2):
+            for side in (LEFT, RIGHT):
+
+                @pl.when(around.has[side])
+                def _(side=side, which=which, i=i):
+                    corner(side, which, i).start()
+
+    for side in (LEFT, RIGHT):
+
+        @pl.when(around.has[side])
+        def _(side=side):
+            beside(side).start()
+
+        @pl.when(jnp.logical_not(around.has[side]))
+        def _(side=side):
+            got_ref[BACK[side] - LEFT] = jnp.zeros(got_ref.shape[1:], BF16)
+
+    for side, target in ((UP, above_ref), (DOWN, below_ref)):
+
+        @pl.when(jnp.logical_not(around.has[side]))
+        def _(target=target):
+            target[...] = jnp.zeros_like(target)
+
+    for i in range(BANDS):
+        for which, part_ref in ((0, up_ref), (1, down_ref)):
+            for side in (LEFT, RIGHT):
+
+                @pl.when(around.has[side])
+                def _(side=side, which=which, i=i):
+                    corner(BACK[side], which, i).wait_recv()
+
+            total = part_ref[pieces[i], :]
+            for back in range(2):
+                total = total + got_ref[back, 2 * which, pieces[i], :].astype(F32)
+            going_ref[which, pieces[i], :] = total.astype(BF16)
+        for side in (UP, DOWN):
+
+            @pl.when(around.has[side])
+            def _(side=side, i=i):
+                vertical(side, i).start()
+
+    for side in (LEFT, RIGHT):
+
+        @pl.when(around.has[side])
+        def _(side=side):
+            beside(BACK[side]).wait_recv()
+
+    own_ref[...] = mid_ref[...] + got_ref[0, 1].astype(F32) + got_ref[1, 1].astype(F32)
+    for side in (LEFT, RIGHT):
+
+        @pl.when(around.has[side])
+        def _(side=side):
+            beside(side).wait_send()
+            for which in range(2):
+                for i in range(BANDS):
+                    corner(side, which, i).wait_send()
+
+    for side in (UP, DOWN):
+
+        @pl.when(around.has[side])
+        def _(side=side):
+            for i in range(BANDS):
+                vertical(side, i).wait_send()
+                vertical(BACK[side], i).wait_recv()
+
+
+def remote_call(kernel, ident, scalars, anys, vectors, outs, spaces, scratch):
+    return pl.pallas_call(
+        kernel,
+        out_shape=outs,
+        in_specs=[pl.BlockSpec(memory_space=pltpu.SMEM)] * len(scalars)
+        + [pl.BlockSpec(memory_space=pl.ANY)] * len(anys)
+        + [pl.BlockSpec(memory_space=pltpu.VMEM)] * len(vectors),
+        out_specs=tuple(pl.BlockSpec(memory_space=space) for space in spaces),
+        scratch_shapes=scratch,
+        compiler_params=pltpu.CompilerParams(
+            vmem_limit_bytes=56 * 1024 * 1024, collective_id=ident, has_side_effects=True
+        ),
+    )(*scalars, *anys, *vectors)
+
+
 def local_call(kernel, scalars, vectors, outs, scratch, flops):
     return pl.pallas_call(
         kernel,
@@ -216,16 +493,7 @@
     length = 2 * size
     slots, slots_uv, block = uv_weight.shape[2], uv_weight.shape[3], uv_weight.shape[4]
     depth = 2 * slots_uv * block
-    up = shifted(sky, "ty", 1)
-    down = shifted(sky, "ty", -1)
-    left = shifted(sky, "tx", 1)
-    right = shifted(sky, "tx", -1)
-    up_left = shifted(up, "tx", 1)
-    up_right = shifted(up, "tx", -1)
-    down_left = shifted(down, "tx", 1)
-    down_right = shifted(down, "tx", -1)
-
-    cos, sin = full_tables(length)
+    cosines, sines = small_tables(length, FINE)
     count = point_count.reshape(1)
     offset = point_offset.reshape(slots, 2)
     bins = jnp.clip(uv_bins.reshape(slots, 2 * slots_uv), 0, length // block - 1)
@@ -244,6 +512,21 @@
     kept = jax.ShapeDtypeStruct((size, size), F32)
     flops = 2 * slots * depth * length * size
 
+    dma = pltpu.SemaphoreType.DMA
+    tile = pltpu.VMEM((size, size), BF16)
+    table = pltpu.VMEM((length, length), BF16)
+    sems = [dma((2, BANDS))] * 2 + [dma((2, 2 * BANDS + 1))] * 2
+    full = jax.ShapeDtypeStruct((length, length), BF16)
+    up_left, left, down_left, up_right, right, down_right, cos, sin, up, down = remote_call(
+        halo_kernel,
+        0,
+        (),
+        (),
+        (cosines, sines, sky),
+        (sent,) * 6 + (full, full, sent, sent),
+        (pl.ANY,) * 8 + (pltpu.VMEM,) * 2,
+        [tile, table, table] + sems + [dma((2,)), dma],
+    )
     early = local_call(
         early_kernel,
         (count, offset, bins, decay),
@@ -265,12 +548,6 @@
         ],
         3 * flops,
     )
-    from_ul = shifted(to_ur, "tx", 1)
-    from_ur = shifted(to_ul, "tx", -1)
-    from_dl = shifted(to_dr, "tx", 1)
-    from_dr = shifted(to_dl, "tx", -1)
-    from_l = shifted(to_r, "tx", 1)
-    from_r = shifted(to_l, "tx", -1)
     to_up, own, to_down = local_call(
         late_kernel,
         (count, offset, bins, decay),
@@ -279,12 +556,17 @@
         [gy, gx, flip],
         flops,
     )
-    to_up = (to_up + from_ul.astype(F32) + from_ur.astype(F32)).astype(BF16)
-    to_down = (to_down + from_dl.astype(F32) + from_dr.astype(F32)).astype(BF16)
-    from_down = shifted(to_up, "ty", -1)
-    from_up = shifted(to_down, "ty", 1)
-    result = own + from_l.astype(F32) + from_r.astype(F32)
-    return result + from_down.astype(F32) + from_up.astype(F32)
+    own, above, below = remote_call(
+        sum_kernel,
+        1,
+        (),
+        (to_ul, to_l, to_dl, to_ur, to_r, to_dr),
+        (to_up, own, to_down),
+        (kept, sent, sent),
+        (pltpu.VMEM,) * 3,
+        [pltpu.VMEM((2, 3, size, size), BF16), pltpu.VMEM((2, size, size), BF16)] + sems,
+    )
+    return own + above.astype(F32) + below.astype(F32)
 
 
 def solution(mesh):

time: 126 us -> 115 us (0.913); the launches traced: 125 us -> 117 us
  Pallas kernels: 26.1 us -> 107 us
  starting transfers between devices: 53.1 us -> 0 us
  waiting for transfers between devices: 20.6 us -> 0 us
  other arithmetic: 21.6 us -> 6.58 us
    pallas_call x0 -> x2, Pallas kernels: none -> 81.2 us  [remote_call(): pl.pallas_call(kernel, out_shape=outs, in_specs=[pl.BlockSpec(memory_spac...]
    ppermute x16 -> x0, starting transfers between devices: 53.1 us -> none  [shifted(): lax.ppermute(value, axis, [(source, source + steps) for source in range(f...]
    ppermute x16 -> x0, waiting for transfers between devices: 20.6 us -> none  [shifted(): lax.ppermute(value, axis, [(source, source + steps) for source in range(f...]
    convert_element_type x3 -> x0, other arithmetic: 19.7 us -> none  [the longest x1 18 us: full_tables(): (jnp.sin(angle) * factor).astype(BF16)]
    mul x0 -> x2, other arithmetic: none -> 1.91 us  [the longest x1 1.91 us: small_tables(): return (jnp.cos(angle) * scale, jnp.sin(angle) * scale)]
    add x1, other arithmetic: 1.35 us -> 2.7 us  [shards(): return own + above.astype(F32) + below.astype(F32)]
  transfers between devices with their start and end apart: 16 -> 0, of which waited for: 3 -> 0; matrix products, arithmetic and copies ran while one was open for 17% -> 0% of each run, Pallas kernels for 11% -> 0%
where the time goes in v2:
time: 115 us; the launch traced here: 117 us
  Pallas kernels  107 us (93%)
  other arithmetic  6.58 us (6%)
  local copies, waits for them, and re-layouts  2.02 us (2%)
    pallas_call x2, Pallas kernels, remote_call(): pl.pallas_call(kernel, out_shape=outs, in_specs=[pl.BlockSpec(memory_spac...  81.2 us
    pallas_call x3, Pallas kernels, local_call(): pl.pallas_call(kernel, out_shape=outs, in_specs=[pl.BlockSpec(memory_spac...  26.1 us
    add x1, other arithmetic, shards(): return own + above.astype(F32) + below.astype(F32)  2.7 us

profile of v2, /device:TPU:21, one launch (start us, length us, event | category | flops | bytes accessed | tf_op | source)
XLA Modules:
  0.0 116.5 jit_solution(16144992812360130883)
XLA Ops:
  0.7 1.2 %fusion.6.decay_ref = f32[4]{0:T(128)} fusion(bf16[1,1,4]{2,1,0:T(2,128)(2,1)} %param.10), kind=kLoop, calls=%fused_computation.15 | loop fusion | flops 16 | bytes 24 | tf_op jit(solution)/shard_map/div | solution.py:502
  1.9 0.1 pad_add_fusion
  1.9 1.3 %copy.10.off_ref = s32[4,2]{1,0:T(4,128)} copy(s32[4,2]{0,1:T(2,128)} %bitcast.12) | data formatting | bytes 64 | tf_op jit(solution)/shard_map/reshape | solution.py:498
  3.3 0.7 broadcast_clamp_fusion
  4.0 0.7 copy.11.bins_ref
  4.6 1.9 %sine_multiply_fusion = (f32[64,1024]{1,0:T(8,128)}, f32[64,1024]{1,0:T(8,128)}) fusion(f32[64]{0:T(128)S(1)} %compare_select_fusion, s32[64]{0:T(128)S(1)} %pad_add_fusion), kind=kLoop, calls=%fused_computation.7 | loop fusion | flops 1048576 | bytes 524800 | tf_op jit(solution)/shard_map/mul | solution.py:27
  6.6 37.1 %shard_map.73 = (bf16[512,512]{1,0:T(8,128)(2,1)}, bf16[512,512]{1,0:T(8,128)(2,1)}, bf16[512,512]{1,0:T(8,128)(2,1)}, bf16[512,512]{1,0:T(8,128)(2,1)}, bf16[51...) custom-call(f32[64,1024]{1,0:T(8,128)} %get-tuple-element.52.cosines, ...), custom_call_target="tpu_custom_call" | custom-call | tf_op jit(solution)/shard_map/pallas_call | solution.py:464
  43.7 6.2 %shard_map.74.early_ref = bf16[4,512,512]{2,1,0:T(8,128)(2,1)} custom-call(s32[1]{0:T(128)} %bitcast.8.count_ref, s32[4,2]{1,0:T(4,128)} %copy.10.off_ref, s32[4,4]{1,0:T(4,128)} %copy.11.bins_ref, f32[4]{0:T(128)} %fusion.6.decay_ref, bf16[1024,1024]{1,0:T(8,128)(2,1)} %get-tuple-element.28.cos_ref, bf16[1024,1024]{1,0:T(8,128)(2,1)} %get-tuple-element.29.sin_ref, ...), custom_call_target="tpu_custom_call" | custom-call | flops 2147483648 | bytes 8388608 | tf_op jit(solution)/shard_map/pallas_call | solution.py:479
  49.8 13.1 %shard_map.75 = (bf16[512,512]{1,0:T(8,128)(2,1)}, bf16[512,512]{1,0:T(8,128)(2,1)}, bf16[512,512]{1,0:T(8,128)(2,1)}, bf16[512,512]{1,0:T(8,128)(2,1)}, bf16[51...) custom-call(s32[1]{0:T(128)} %bitcast.9.count_ref, s32[4,2]{1,0:T(4,128)} %copy.10.off_ref, ...), custom_call_target="tpu_custom_call" | custom-call | flops 6442450944 | bytes 8388608 | tf_op jit(solution)/shard_map/pallas_call | solution.py:479
  62.9 6.8 %shard_map.76 = (f32[512,512]{1,0:T(8,128)}, f32[512,512]{1,0:T(8,128)}, f32[512,512]{1,0:T(8,128)}) custom-call(s32[1]{0:T(128)} %bitcast.10.count_ref, s32[4,2]{1,0:T(4,128)} %copy.10.off_ref, s32[4,4]{1,0:T(4,128)} %copy.11.bins_ref, f32[4]{0:T(128)} %fusion.6.decay_ref, bf16[1024,1024]{1,0:T(8,128)(2,1)} %get-tuple-element.28.cos_ref, ...), custom_call_target="tpu_custom_call" | custom-call | flops 2147483648 | bytes 8388608 | tf_op jit(solution)/shard_map/pallas_call | solution.py:479
  69.8 44.1 %shard_map.77 = (f32[512,512]{1,0:T(8,128)}, bf16[512,512]{1,0:T(8,128)(2,1)}, bf16[512,512]{1,0:T(8,128)(2,1)}) custom-call(bf16[512,512]{1,0:T(8,128)(2,1)} %get-tuple-element.38.ul_ref, bf16[512,512]{1,0:T(8,128)(2,1)} %get-tuple-element.39.l_ref, bf16[512,512]{1,0:T(8,128)(2,1)} %get-tuple-element.40.dl_ref, bf16[512,512]{1,0:T(8,128)(2,1)} %get-tuple-element.41.ur_ref, ...), custom_call_target="tpu_custom_call" | custom-call | tf_op jit(solution)/shard_map/pallas_call | solution.py:464
  113.8 2.7 %convert_add_fusion = f32[512,512]{1,0:T(8,128)} fusion(bf16[512,512]{1,0:T(8,128)(2,1)} %get-tuple-element.50, f32[512,512]{1,0:T(8,128)} %get-tuple-element.48, bf16[512,512]{1,0:T(8,128)(2,1)} %get-tuple-element.49), kind=kLoop, calls=%fused_computation | loop fusion | flops 1048576 | bytes 3145728 | tf_op jit(solution)/shard_map/add | solution.py:569
  (3 shorter events, 0.0 us)
